TPU v7x, 16 devices: a whole 2x2x2 slice. The times are simulated.
16 devices in a mesh: terms: 16 (over z, y, x, core).
Axes of the slice: x: 2, y: 2, z: 2, core: 2. Of those that a mesh axis runs over, the one named last changes fastest.
Arguments:
- wavefunction: float32 [640, 16, 640], replicated
- left_env: bfloat16 [32, 640, 640], P('terms')
- pair_ops: bfloat16 [32, 16, 16], P('terms')
- right_env: bfloat16 [32, 640, 640], P('terms')
- full_term: int32 [32], P('terms')
Outputs:
- output 1: float32 [7, 640, 16, 640], P(None, 'terms')
- output 2: float32 [6], replicated
- output 3: float32 [6], replicated
All inputs are finite; a program needn't handle non-finite values.
Results may differ from a plain program's by a relative error of at most 0.011385.
Values are sent between devices in bfloat16 or wider.
A program may use at most 1 GiB of HBM per device.

v0:
```python
import jax
import jax.numpy as jnp
from jax import lax
from jax.sharding import PartitionSpec as P

LANCZOS_STEPS = 6
AXIS_NAME = 'terms'


def local_sigma(vec_bf, left_loc, pair_loc, right_loc, flag_loc):
    def apply_right(right_env):
        return lax.dot_general(vec_bf, right_env, (((2,), (1,)), ((), ())), preferred_element_type=jnp.float32).astype(jnp.bfloat16)

    def keep_vector(right_env):
        return vec_bf

    def term_body(term_idx, running_sum):
        right_done = lax.cond(flag_loc[term_idx] == 1, apply_right, keep_vector, right_loc[term_idx])
        pair_done = lax.dot_general(pair_loc[term_idx], right_done, (((1,), (1,)), ((), ())), preferred_element_type=jnp.float32).astype(jnp.bfloat16)
        return running_sum + lax.dot_general(left_loc[term_idx], pair_done, (((1,), (1,)), ((), ())), preferred_element_type=jnp.float32)

    start_sum = jnp.zeros(vec_bf.shape, jnp.float32)
    return lax.fori_loop(0, left_loc.shape[0], term_body, start_sum)


def solution(mesh):
    group_size = mesh.shape[AXIS_NAME]

    def device_body(wavefunction, left_loc, pair_loc, right_loc, flag_loc):
        bond_dim = wavefunction.shape[0]
        vec_size = wavefunction.size
        slab_rows = bond_dim // group_size
        row_start = lax.axis_index(AXIS_NAME) * slab_rows
        first_vec = wavefunction / jnp.sqrt(jnp.sum(wavefunction * wavefunction) / vec_size)
        whole_bf = first_vec.astype(jnp.bfloat16)
        current = lax.dynamic_slice_in_dim(first_vec, row_start, slab_rows, axis=0)
        previous = jnp.zeros_like(current)
        beta_prev = jnp.zeros((), jnp.float32)
        slab_list = [current]
        alpha_list = []
        beta_list = []
        for step_num in range(LANCZOS_STEPS):
            part_sigma = local_sigma(whole_bf, left_loc, pair_loc, right_loc, flag_loc)
            sigma_slab = lax.psum_scatter(part_sigma, AXIS_NAME, scatter_dimension=0, tiled=True)
            alpha_now = lax.psum(jnp.sum(sigma_slab * current), AXIS_NAME) / vec_size
            residual = sigma_slab - alpha_now * current - beta_prev * previous
            beta_now = jnp.sqrt(lax.psum(jnp.sum(residual * residual), AXIS_NAME) / vec_size)
            following = residual / beta_now
            slab_list.append(following)
            alpha_list.append(alpha_now)
            beta_list.append(beta_now)
            if step_num + 1 < LANCZOS_STEPS:
                whole_bf = lax.all_gather(following.astype(jnp.bfloat16), AXIS_NAME, axis=0, tiled=True)
            previous, current, beta_prev = current, following, beta_now
        return jnp.stack(slab_list), jnp.stack(alpha_list), jnp.stack(beta_list)

    return jax.shard_map(device_body, mesh=mesh, in_specs=(P(), P(AXIS_NAME), P(AXIS_NAME), P(AXIS_NAME), P(AXIS_NAME)), out_specs=(P(None, AXIS_NAME), P(), P()), check_vma=False)
```

profile of v0, /device:TPU:0, one launch (start us, length us, event | category | flops | bytes accessed | tf_op | source)
XLA Modules:
  0.0 3719.6 jit_solution(3869487904262289345)
XLA Ops:
  47.1 130.2 %while.84 = (s32[]{:T(128)}, f32[640,16,640]{2,0,1:T(8,128)}, bf16[2,640,640]{2,1,0:T(8,128)(2,1)S(1)}, bf16[2,16,16]{2,1,0:T(8,128)(2,1)S(1)}, s32[2]{0:T(128)S...) while((s32[]{:T(128)}, f32[640,16,640]{2,0,1:T(8,128)}, ...), condition=%wide.region_4.0_spmd.clone, body=%wide.region_1.0_spmd.clone.sunk | while | flops 17013145600 | bytes 145821888 | solution.py:23
  48.5 23.3 conditional.18
  48.5 23.3 copy.74
  84.8 25.7 select_add_fusion.12
  111.7 23.3 conditional.18
  111.7 23.3 copy.74
  148.0 28.9 select_add_fusion.12
  177.3 32.7 copy.63
  210.0 314.7 %reduce-scatter.7.cloned.1.call-done = f32[40,16,640]{2,1,0:T(8,128)} async-done(((f32[640,16,640]{2,1,0:T(8,128)}), f32[40,16,640]{2,1,0:T(8,128)}) %reduce-scatter.7.cloned.1.call-update) | async-done | bytes 1638416 | tf_op jit(solution)/shard_map/reduce_scatter | solution.py:44
  527.7 31.0 psum.84
  562.3 32.7 psum.85
  599.4 65.0 %all-gather.6.cloned.1.call-done = bf16[640,16,640]{2,1,0:T(8,128)(2,1)} async-done(((bf16[40,16,640]{2,1,0:T(8,128)(2,1)}), bf16[640,16,640]{2,1,0:T(8,128)(2,1)}) %all-gather.6.cloned.1.call-update) | async-done | bytes 13107216 | tf_op jit(solution)/shard_map/all_gather | solution.py:53
  676.6 130.1 %while.85 = (s32[]{:T(128)}, f32[640,16,640]{2,0,1:T(8,128)}, bf16[2,640,640]{2,1,0:T(8,128)(2,1)S(1)}, bf16[2,16,16]{2,1,0:T(8,128)(2,1)S(1)}, s32[2]{0:T(128)S...) while((s32[]{:T(128)}, f32[640,16,640]{2,0,1:T(8,128)}, ...), condition=%wide.region_13.0_spmd.clone, body=%wide.region_10.0_spmd.clone.sunk | while | flops 17013145600 | bytes 145821888 | solution.py:23
  678.0 23.3 conditional.19
  678.1 23.3 copy.77
  714.3 25.7 select_add_fusion.13
  741.2 23.3 conditional.19
  741.2 23.3 copy.77
  777.5 28.9 select_add_fusion.13
  806.8 33.3 copy.65
  840.2 311.9 %reduce-scatter.9.cloned.1.call-done = f32[40,16,640]{2,1,0:T(8,128)} async-done(((f32[640,16,640]{2,1,0:T(8,128)}), f32[40,16,640]{2,1,0:T(8,128)}) %reduce-scatter.9.cloned.1.call-update) | async-done | bytes 1638416 | tf_op jit(solution)/shard_map/reduce_scatter | solution.py:44
  1154.5 31.0 psum.86
  1189.6 32.7 psum.87
  1224.2 64.9 %all-gather.8.cloned.1.call-done = bf16[640,16,640]{2,1,0:T(8,128)(2,1)} async-done(((bf16[40,16,640]{2,1,0:T(8,128)(2,1)}), bf16[640,16,640]{2,1,0:T(8,128)(2,1)}) %all-gather.8.cloned.1.call-update) | async-done | bytes 13107216 | tf_op jit(solution)/shard_map/all_gather | solution.py:53
  1301.4 130.2 %while.86 = (s32[]{:T(128)}, f32[640,16,640]{2,0,1:T(8,128)}, bf16[2,640,640]{2,1,0:T(8,128)(2,1)S(1)}, bf16[2,16,16]{2,1,0:T(8,128)(2,1)S(1)}, s32[2]{0:T(128)S...) while((s32[]{:T(128)}, f32[640,16,640]{2,0,1:T(8,128)}, ...), condition=%wide.region_22.0_spmd.clone, body=%wide.region_19.0_spmd.clone.sunk | while | flops 17013145600 | bytes 145822400 | solution.py:23
  1302.8 23.3 conditional.20
  1302.8 23.3 copy.80
  1339.1 25.7 select_add_fusion.14
  1366.0 23.3 conditional.20
  1402.3 28.9 select_add_fusion.14
  1431.6 32.7 copy.67
  1464.4 302.2 %reduce-scatter.11.cloned.1.call-done = f32[40,16,640]{2,1,0:T(8,128)} async-done(((f32[640,16,640]{2,1,0:T(8,128)}), f32[40,16,640]{2,1,0:T(8,128)}) %reduce-scatter.11.cloned.1.call-update) | async-done | bytes 1638416 | tf_op jit(solution)/shard_map/reduce_scatter | solution.py:44
  1769.1 31.0 psum.88
  1804.8 32.7 psum.89
  1840.8 64.9 %all-gather.10.cloned.1.call-done = bf16[640,16,640]{2,1,0:T(8,128)(2,1)} async-done(((bf16[40,16,640]{2,1,0:T(8,128)(2,1)}), bf16[640,16,640]{2,1,0:T(8,128)(2,1)}) %all-gather.10.cloned.1.call-update) | async-done | bytes 13107216 | tf_op jit(solution)/shard_map/all_gather | solution.py:53
  1918.0 130.1 %while.87 = (s32[]{:T(128)}, f32[640,16,640]{2,0,1:T(8,128)}, bf16[2,640,640]{2,1,0:T(8,128)(2,1)S(1)}, bf16[2,16,16]{2,1,0:T(8,128)(2,1)S(1)}, s32[2]{0:T(128)S...) while((s32[]{:T(128)}, f32[640,16,640]{2,0,1:T(8,128)}, ...), condition=%wide.region_31.0_spmd.clone, body=%wide.region_28.0_spmd.clone.sunk | while | flops 17013145600 | bytes 145821888 | solution.py:23
  1919.4 23.3 conditional.21
  1955.7 25.7 select_add_fusion.15
  1982.6 23.3 conditional.21
  2018.8 28.9 select_add_fusion.15
  2048.1 32.7 copy.69
  2080.9 311.9 %reduce-scatter.13.cloned.1.call-done = f32[40,16,640]{2,1,0:T(8,128)} async-done(((f32[640,16,640]{2,1,0:T(8,128)}), f32[40,16,640]{2,1,0:T(8,128)}) %reduce-scatter.13.cloned.1.call-update) | async-done | bytes 1638416 | tf_op jit(solution)/shard_map/reduce_scatter | solution.py:44
  2395.8 31.0 psum.90
  2431.6 32.7 psum.91
  2467.6 65.0 %all-gather.12.cloned.1.call-done = bf16[640,16,640]{2,1,0:T(8,128)(2,1)} async-done(((bf16[40,16,640]{2,1,0:T(8,128)(2,1)}), bf16[640,16,640]{2,1,0:T(8,128)(2,1)}) %all-gather.12.cloned.1.call-update) | async-done | bytes 13107216 | tf_op jit(solution)/shard_map/all_gather | solution.py:53
  2544.8 130.3 %while.88 = (s32[]{:T(128)}, f32[640,16,640]{2,0,1:T(8,128)}, bf16[2,640,640]{2,1,0:T(8,128)(2,1)S(1)}, bf16[2,16,16]{2,1,0:T(8,128)(2,1)S(1)}, s32[2]{0:T(128)S...) while((s32[]{:T(128)}, f32[640,16,640]{2,0,1:T(8,128)}, ...), condition=%wide.region_40.0_spmd.clone, body=%wide.region_37.0_spmd.clone.sunk | while | flops 17013145600 | bytes 145822400 | solution.py:23
  2546.3 23.3 conditional.22
  2582.5 25.7 select_add_fusion.16
  2609.5 23.3 conditional.22
  2645.8 28.9 select_add_fusion.16
  2675.1 32.7 copy.71
  2707.9 302.3 %reduce-scatter.15.cloned.1.call-done = f32[40,16,640]{2,1,0:T(8,128)} async-done(((f32[640,16,640]{2,1,0:T(8,128)}), f32[40,16,640]{2,1,0:T(8,128)}) %reduce-scatter.15.cloned.1.call-update) | async-done | bytes 1638416 | tf_op jit(solution)/shard_map/reduce_scatter | solution.py:44
  3013.1 31.0 psum.92
  3048.8 32.7 psum.93
  3084.8 65.0 %all-gather.14.cloned.1.call-done = bf16[640,16,640]{2,1,0:T(8,128)(2,1)} async-done(((bf16[40,16,640]{2,1,0:T(8,128)(2,1)}), bf16[640,16,640]{2,1,0:T(8,128)(2,1)}) %all-gather.14.cloned.1.call-update) | async-done | bytes 13107216 | tf_op jit(solution)/shard_map/all_gather | solution.py:53
  3162.0 130.0 %while.89 = (s32[]{:T(128)}, f32[640,16,640]{2,0,1:T(8,128)}, bf16[2,640,640]{2,1,0:T(8,128)(2,1)S(1)}, bf16[2,16,16]{2,1,0:T(8,128)(2,1)S(1)}, s32[2]{0:T(128)S...) while((s32[]{:T(128)}, f32[640,16,640]{2,0,1:T(8,128)}, ...), condition=%wide.region_49.0_spmd.clone, body=%wide.region_46.0_spmd.clone.sunk | while | flops 17013145600 | bytes 145821888 | solution.py:23
  3163.4 23.3 conditional.23
  3199.7 25.7 select_add_fusion.17
  3226.6 23.3 conditional.23
  3262.9 29.0 select_add_fusion.17
  3292.1 32.7 copy.73
  3334.2 302.5 %reduce-scatter.17.cloned.1.call-done = f32[40,16,640]{2,1,0:T(8,128)} async-done(((f32[640,16,640]{2,1,0:T(8,128)}), f32[40,16,640]{2,1,0:T(8,128)}) %reduce-scatter.17.cloned.1.call-update) | async-done | bytes 1638416 | tf_op jit(solution)/shard_map/reduce_scatter | solution.py:44
  3642.3 31.0 psum.94
  3676.9 32.7 psum.95
  (129 shorter events, 492.4 us)
Async XLA Ops:
  7.2 517.6 %reduce-scatter.7.cloned.1.call-start = ((), (), s32[]{:S(2)}) async-start(), calls=%async_computation.6 | async-start | bytes 27852800 | tf_op jit(solution)/shard_map/reduce_scatter | solution.py:44
  38.3 8.7 copy-start
  38.3 8.7 copy-start.10
  38.3 8.7 copy-start.13
  38.3 8.7 copy-start.17
  210.0 454.4 %all-gather.6.cloned.1.call-start = ((), (), s32[]{:S(2)}) async-start(), calls=%async_computation.7 | async-start | bytes 13926400 | tf_op jit(solution)/shard_map/all_gather | solution.py:53
  599.3 552.7 %reduce-scatter.9.cloned.1.call-start = ((), (), s32[]{:S(2)}) async-start(), calls=%async_computation.8 | async-start | bytes 27852800 | tf_op jit(solution)/shard_map/reduce_scatter | solution.py:44
  806.8 33.3 copy-start.11
  806.8 33.3 copy-start.14
  840.1 312.0 %copy-start.9 = (f32[40,16,640]{2,1,0:T(8,128)S(1)}, f32[40,16,640]{2,1,0:T(8,128)}, u32[]{:S(2)}) copy-start(f32[40,16,640]{2,1,0:T(8,128)} %get-tuple-element.1286) | copy-start | bytes 4915204
  840.1 449.0 %all-gather.8.cloned.1.call-start = ((), (), s32[]{:S(2)}) async-start(), calls=%async_computation.9 | async-start | bytes 13926400 | tf_op jit(solution)/shard_map/all_gather | solution.py:53
  1189.6 111.7 %copy-start.1 = (f32[40,16,640]{2,1,0:T(8,128)}, f32[40,16,640]{2,1,0:T(8,128)S(1)}, u32[]{:S(2)}) copy-start(f32[40,16,640]{2,1,0:T(8,128)S(1)} %get-tuple-element.1284) | copy-start | bytes 4915204
  1224.1 542.5 %reduce-scatter.11.cloned.1.call-start = ((), (), s32[]{:S(2)}) async-start(), calls=%async_computation.10 | async-start | bytes 27852800 | tf_op jit(solution)/shard_map/reduce_scatter | solution.py:44
  1224.2 77.2 %copy-start.12 = (bf16[2,16,16]{2,1,0:T(8,128)(2,1)S(1)}, bf16[2,16,16]{2,1,0:T(8,128)(2,1)}, u32[]{:S(2)}) copy-start(bf16[2,16,16]{2,1,0:T(8,128)(2,1)} %copy-done.11) | copy-start | bytes 3076
  1464.3 302.3 %copy-start.2 = (f32[40,16,640]{2,1,0:T(8,128)S(1)}, f32[40,16,640]{2,1,0:T(8,128)}, u32[]{:S(2)}) copy-start(f32[40,16,640]{2,1,0:T(8,128)} %copy-done.1) | copy-start | bytes 4915204
  1464.3 441.4 %all-gather.10.cloned.1.call-start = ((), (), s32[]{:S(2)}) async-start(), calls=%async_computation.11 | async-start | bytes 13926400 | tf_op jit(solution)/shard_map/all_gather | solution.py:53
  1840.7 552.1 %reduce-scatter.13.cloned.1.call-start = ((), (), s32[]{:S(2)}) async-start(), calls=%async_computation.12 | async-start | bytes 27852800 | tf_op jit(solution)/shard_map/reduce_scatter | solution.py:44
  1840.8 77.2 %copy-start.15 = (bf16[2,640,640]{2,1,0:T(8,128)(2,1)S(1)}, bf16[2,640,640]{2,1,0:T(8,128)(2,1)}, u32[]{:S(2)}) copy-start(bf16[2,640,640]{2,1,0:T(8,128)(2,1)} %get-tuple-element.1807) | copy-start | bytes 4915204
  2080.8 346.6 %copy-start.3 = (f32[40,16,640]{2,1,0:T(8,128)S(1)}, f32[40,16,640]{2,1,0:T(8,128)}, u32[]{:S(2)}) copy-start(f32[40,16,640]{2,1,0:T(8,128)} %copy-done.1) | copy-start | bytes 4915204
  2080.8 451.7 %all-gather.12.cloned.1.call-start = ((), (), s32[]{:S(2)}) async-start(), calls=%async_computation.13 | async-start | bytes 13926400 | tf_op jit(solution)/shard_map/all_gather | solution.py:53
  2467.5 542.6 %reduce-scatter.15.cloned.1.call-start = ((), (), s32[]{:S(2)}) async-start(), calls=%async_computation.14 | async-start | bytes 27852800 | tf_op jit(solution)/shard_map/reduce_scatter | solution.py:44
  2707.8 336.9 %copy-start.5 = (f32[40,16,640]{2,1,0:T(8,128)S(1)}, f32[40,16,640]{2,1,0:T(8,128)}, u32[]{:S(2)}) copy-start(f32[40,16,640]{2,1,0:T(8,128)} %get-tuple-element.1282) | copy-start | bytes 4915204
  2707.8 441.9 %all-gather.14.cloned.1.call-start = ((), (), s32[]{:S(2)}) async-start(), calls=%async_computation.15 | async-start | bytes 13926400 | tf_op jit(solution)/shard_map/all_gather | solution.py:53
  3084.7 551.9 %reduce-scatter.17.cloned.1.call-start = ((), (), s32[]{:S(2)}) async-start(), calls=%async_computation.16 | async-start | bytes 27852800 | tf_op jit(solution)/shard_map/reduce_scatter | solution.py:44
  3084.8 77.3 %copy-start.16 = (bf16[2,640,640]{2,1,0:T(8,128)(2,1)S(1)}, bf16[2,640,640]{2,1,0:T(8,128)(2,1)}, u32[]{:S(2)}) copy-start(bf16[2,640,640]{2,1,0:T(8,128)(2,1)} %get-tuple-element.1809) | copy-start | bytes 4915204
  3324.8 5.6 copy-start.4
  3324.8 6.9 copy-start.6
  3324.8 8.1 copy-start.7
  3331.6 342.3 %copy-start.8 = (f32[40,16,640]{2,1,0:T(8,128)S(1)}, f32[40,16,640]{2,1,0:T(8,128)}, u32[]{:S(2)}) copy-start(f32[40,16,640]{2,1,0:T(8,128)} %get-tuple-element.1280) | copy-start | bytes 4915204
Sparse Core Ops, SparseCore 0:
  210.1 314.6 reduce-scatter.6
  599.5 64.8 all-gather.5
  840.3 311.7 reduce-scatter.8
  1224.2 64.8 all-gather.7
  1464.5 302.1 reduce-scatter.10
  1840.8 64.8 all-gather.9
  2081.0 311.8 reduce-scatter.12
  2467.6 64.8 all-gather.11
  2707.9 302.1 reduce-scatter.14
  3084.8 64.8 all-gather.13
  3324.9 311.7 reduce-scatter.16
where the time goes:
time: 3730 us; the launch traced here: 3720 us
  waiting for transfers between devices  2170 us (58%)
  local copies, waits for them, and re-layouts  560 us (15%)
  matrix products  483 us (13%)
  blocking collectives  382 us (10%)
  other arithmetic  88.7 us (2%)
    reduce_scatter x6, waiting for transfers between devices, device_body(): lax.psum_scatter(part_sigma, AXIS_NAME, scatter_dimension=0, tiled=True)  1850 us
    dot_general x12, matrix products, term_body(): lax.dot_general(left_loc[term_idx], pair_done, (((1,), (1,)), ((), ())),...  327 us
    all_gather x5, waiting for transfers between devices, device_body(): lax.all_gather(following.astype(jnp.bfloat16), AXIS_NAME, axis=0, tiled=T...  325 us
    cond x12, local copies, waits for them, and re-layouts, term_body(): lax.cond(flag_loc[term_idx] == 1, apply_right, keep_vector, right_loc[ter...  279 us
    while x6, local copies, waits for them, and re-layouts, local_sigma(): return lax.fori_loop(0, left_loc.shape[0], term_body, start_sum)  197 us
    psum x6, blocking collectives, device_body(): lax.psum(jnp.sum(residual * residual), AXIS_NAME) / vec_size  196 us
    psum x6, blocking collectives, device_body(): alpha_now = lax.psum(jnp.sum(sigma_slab * current), AXIS_NAME) / vec_size  186 us
    dot_general x12, matrix products, term_body(): lax.dot_general(pair_loc[term_idx], right_done, (((1,), (1,)), ((), ())),...  156 us
  transfers between devices with their start and end apart: 11, of which 11 were waited for; matrix products, arithmetic and copies ran while one was open for 0% of the time, Pallas kernels for 0%

commit v1 on v0

v1 whole, which is shorter than its diff:
```python
import functools
import jax
import jax.numpy as jnp
from jax import lax
from jax.experimental import pallas as pl
from jax.sharding import PartitionSpec as P
from jax.experimental.pallas import tpu as pltpu

LANCZOS_STEPS = 6
AXIS_NAME = 'terms'
BOND = 640
PAIR = 16
TERMS = 32
DEVS = 16
SLAB = BOND // DEVS
CHUNKS = 5
LANES = 128
VEC_SIZE = BOND * PAIR * BOND
bf = jnp.bfloat16
f32 = jnp.float32
MESH = pl.DeviceIdType.MESH
PART_PAIRS = ((0, 3), (3, 6), (6, 8))
PART_AXES = ((0, 1, 2), (1, 2, 0), (2, 0, 1))


def lanczos_kernel(psi_hbm, rc, wi, left_hbm, krylov, alphas, betas, u, lft, y, zb, acc, cur, prev, ar,
                   load_sem, out_sem, ici_send, ici_recv, d2d_send, d2d_recv, ar_send, ar_recv):
    me = lax.axis_index(AXIS_NAME)
    core = lax.rem(me, 2)
    place = (lax.rem(me // 2, 2), lax.rem(me // 4, 2), me // 8)
    across = tuple(me + (2 << n) * (1 - 2 * place[n]) for n in range(3))
    partner = me + 1 - 2 * core

    def view(ch, pairs, gathered, flipped=None):
        idx = []
        for n in (2, 1, 0):
            if n in gathered:
                idx.append(slice(None))
            elif n == flipped:
                idx.append(1 - place[n])
            else:
                idx.append(place[n])
        return u.at[(ch, slice(pairs[0], pairs[1])) + tuple(idx) + (core,)]

    def remote(ref, dst_ref, send, recv, dev):
        return pltpu.make_async_remote_copy(src_ref=ref, dst_ref=dst_ref, send_sem=send, recv_sem=recv, device_id=(dev,), device_id_type=MESH)

    def ici(ch, part, stage):
        axes = PART_AXES[part]
        ref = view(ch, PART_PAIRS[part], axes[:stage])
        return remote(ref, ref, ici_send.at[ch, part, stage], ici_recv.at[ch, part, stage], across[axes[stage]])

    def ici_in(ch, part, stage):
        axes = PART_AXES[part]
        ref = view(ch, PART_PAIRS[part], axes[:stage], axes[stage])
        return remote(ref, ref, ici_send.at[ch, part, stage], ici_recv.at[ch, part, stage], across[axes[stage]])

    def d2d(ch, part, stage):
        axes = PART_AXES[part]
        ref = view(ch, PART_PAIRS[part], axes[:stage], axes[stage])
        return remote(ref, ref, d2d_send.at[ch, 3 * part + stage], d2d_recv.at[ch, 3 * part + stage], partner)

    def d2d_own(ch):
        ref = view(ch, (0, 8), ())
        return remote(ref, ref, d2d_send.at[ch, 9], d2d_recv.at[ch, 9], partner)

    def first_sends(ch):
        for part in range(3):
            ici(ch, part, 0).start()
        d2d_own(ch).start()

    def forward(ch, stage):
        for part in range(3):
            ici_in(ch, part, stage).wait_recv()
            if stage < 2:
                ici(ch, part, stage + 1).start()
            d2d(ch, part, stage).start()

    def chunk_ready(ch):
        for part in range(3):
            for stage in range(3):
                d2d(ch, part, stage).wait_recv()
        d2d_own(ch).wait_recv()

    def drain_sends(ch):
        for part in range(3):
            for stage in range(3):
                ici(ch, part, stage).wait_send()
                d2d(ch, part, stage).wait_send()
        d2d_own(ch).wait_send()

    def all_sum(which, partial):
        ar[which, me] = partial
        for off in range(1, DEVS):
            dev = lax.rem(me + off, DEVS)
            ref = ar.at[which, me]
            remote(ref, ref, ar_send.at[which, off], ar_recv.at[which, me], dev).start()
        for off in range(1, DEVS):
            dev = lax.rem(me + off, DEVS)
            ref = ar.at[which, dev]
            remote(ref, ref, ar_send.at[which, off], ar_recv.at[which, dev], dev).wait_recv()
        total = jnp.sum(jnp.sum(ar[which], axis=0))
        for off in range(1, DEVS):
            dev = lax.rem(me + off, DEVS)
            ref = ar.at[which, me]
            remote(ref, ref, ar_send.at[which, off], ar_recv.at[which, me], dev).wait_send()
        return total

    def fold(vals):
        return jnp.sum(vals.reshape(80, 8, 5, 128).transpose(0, 2, 1, 3).reshape(400, 8, 128), axis=0)

    def dot_rows(fn):
        def body(g, tot):
            rows = pl.ds(pl.multiple_of(g * 16, 16), 16)
            val = fn(rows)
            for r in range(2):
                for c in range(5):
                    tot = tot + val[8 * r:8 * r + 8, 128 * c:128 * c + 128]
            return tot
        return lax.fori_loop(0, 40, body, jnp.zeros((8, 128), f32))

    def write_u():
        for ch in range(CHUNKS):
            lanes = slice(128 * ch, 128 * ch + 128)
            for i in range(8):
                dst = u.at[ch, i, place[2], place[1], place[0], core]
                dst[0:16] = cur[32 * i:32 * i + 16, lanes].astype(bf)
                dst[16:32] = cur[256 + 32 * i:256 + 32 * i + 16, lanes].astype(bf)
                dst[32:48] = cur[32 * i + 16:32 * i + 32, lanes].astype(bf)
                dst[48:64] = cur[256 + 32 * i + 16:256 + 32 * i + 32, lanes].astype(bf)
                dst[64:80] = cur[512 + 16 * i:512 + 16 * i + 16, lanes].astype(bf)

    def right_phase(ch):
        @pl.loop(0, 2)
        def _(g):
            for par in range(2):
                rhs = []
                for n in range(4):
                    i = g * 4 + n
                    a = u[ch, i, :, :, :, :, 32 * par:32 * par + 32, :].reshape(512, 128)
                    m = u[ch, i, :, :, :, :, 64:80, :].reshape(256, 128)
                    rhs.append(jnp.concatenate([a, m], axis=0))
                rhs = jnp.concatenate(rhs, axis=1)
                lhs = jnp.concatenate([rc[:, 0:512], rc[:, 512 + 256 * par:768 + 256 * par]], axis=1)
                o = jnp.dot(lhs, rhs, preferred_element_type=f32).astype(bf)
                for n in range(4):
                    y[2 * (g * 4 + n) + par] = o[:, 128 * n:128 * n + 128]

    def pair_left_phase(ch, groups):
        @pl.loop(*groups)
        def _(kg):
            for s in range(2):
                k = kg * 2 + s
                row = pl.multiple_of(k * 80, 16)
                tile = [y[:, pl.ds(row + 16 * t, 16), :].reshape(256, 128) for t in range(5)]
                z01 = jnp.dot(wi[k, 0], jnp.concatenate([tile[0], tile[1]], axis=1), preferred_element_type=f32).astype(bf)
                z2 = jnp.dot(wi[k, 1], tile[2], preferred_element_type=f32).reshape(16, 2, 8, 128)
                z34 = jnp.dot(wi[k, 2], jnp.concatenate([tile[3], tile[4]], axis=1), preferred_element_type=f32).astype(bf)
                zb[s, 0:256, 0:128] = z01[:, 0:128]
                zb[s, 256:512, 0:128] = z01[:, 128:256]
                zb[s, 512:640, 0:128] = z2[:, 0].reshape(128, 128).astype(bf)
                zb[s, 0:256, 128:256] = z34[:, 0:128]
                zb[s, 256:512, 128:256] = z34[:, 128:256]
                zb[s, 512:640, 128:256] = z2[:, 1].reshape(128, 128).astype(bf)
            lhs = jnp.concatenate([zb[0], zb[1]], axis=1)
            c0 = pl.multiple_of(ch * 128, 128)
            rhs = jnp.concatenate([lft[kg * 4 + n, pl.ds(c0, 128), :] for n in range(4)], axis=0)
            acc[...] += jnp.dot(lhs, rhs, preferred_element_type=f32)

    left_load = pltpu.make_async_copy(left_hbm, lft, load_sem.at[0])
    left_load.start()
    psi_load = pltpu.make_async_copy(psi_hbm, cur, load_sem.at[1])
    psi_load.start()
    barrier = pltpu.get_barrier_semaphore()
    for off in range(1, DEVS):
        pl.semaphore_signal(barrier, inc=1, device_id=(lax.rem(me + off, DEVS),), device_id_type=MESH)
    pl.semaphore_wait(barrier, DEVS - 1)
    psi_load.wait()
    norm = jnp.sqrt(all_sum(1, dot_rows(lambda rows: cur[rows, :] * cur[rows, :])) / VEC_SIZE)
    betas[0, LANCZOS_STEPS] = norm
    prev[...] = jnp.zeros_like(prev)

    @pl.loop(0, 40)
    def _(g):
        rows = pl.ds(pl.multiple_of(g * 16, 16), 16)
        cur[rows, :] = cur[rows, :] / norm

    write_u()
    left_load.wait()

    def step(j, beta_prev):
        acc[...] = jnp.zeros_like(acc)
        first_sends(0)
        first_sends(1)
        forward(0, 0)
        first_sends(2)
        forward(0, 1)
        forward(1, 0)
        forward(0, 2)
        chunk_ready(0)

        @pl.loop(0, CHUNKS)
        def _(ch):
            @pl.when(ch + 1 < CHUNKS)
            def _():
                forward(ch + 1, 1)

            @pl.when(ch + 2 < CHUNKS)
            def _():
                forward(ch + 2, 0)

            @pl.when(ch + 3 < CHUNKS)
            def _():
                first_sends(ch + 3)

            right_phase(ch)
            pair_left_phase(ch, (0, 4))

            @pl.when(ch + 1 < CHUNKS)
            def _():
                forward(ch + 1, 2)

            pair_left_phase(ch, (4, 8))

            @pl.when(ch + 1 < CHUNKS)
            def _():
                chunk_ready(ch + 1)

        @pl.loop(0, CHUNKS)
        def _(ch):
            drain_sends(ch)

        alpha = all_sum(0, dot_rows(lambda rows: acc[rows, :] * cur[rows, :])) / VEC_SIZE

        def residual(rows):
            w = acc[rows, :] - alpha * cur[rows, :] - beta_prev * prev[rows, :]
            acc[rows, :] = w
            return w * w

        beta = jnp.sqrt(all_sum(1, dot_rows(residual)) / VEC_SIZE)
        alphas[0, j] = alpha
        betas[0, j] = beta

        @pl.when(j > 0)
        def _():
            pltpu.make_async_copy(cur, krylov.at[0], out_sem).wait()

        @pl.loop(0, 40)
        def _(g):
            rows = pl.ds(pl.multiple_of(g * 16, 16), 16)
            prev[rows, :] = cur[rows, :]
            cur[rows, :] = acc[rows, :] / beta

        pltpu.make_async_copy(cur, krylov.at[j], out_sem).start()

        @pl.when(j + 1 < LANCZOS_STEPS)
        def _():
            write_u()

        return beta

    lax.fori_loop(0, LANCZOS_STEPS, step, jnp.zeros((), f32))
    pltpu.make_async_copy(cur, krylov.at[0], out_sem).wait()


def run_lanczos(psi_slab, rc, wi, left_all):
    vmem = pl.BlockSpec(memory_space=pltpu.VMEM)
    smem = pl.BlockSpec(memory_space=pltpu.SMEM)
    hbm = pl.BlockSpec(memory_space=pltpu.HBM)
    dma = pltpu.SemaphoreType.DMA
    return pl.pallas_call(
        lanczos_kernel,
        out_shape=(jax.ShapeDtypeStruct((LANCZOS_STEPS, BOND, BOND), f32), jax.ShapeDtypeStruct((1, 8), f32), jax.ShapeDtypeStruct((1, 8), f32)),
        in_specs=[hbm, vmem, vmem, hbm],
        out_specs=(hbm, smem, smem),
        scratch_shapes=[
            pltpu.VMEM((CHUNKS, 8, 2, 2, 2, 2, 80, LANES), bf),
            pltpu.VMEM((TERMS, BOND, BOND), bf),
            pltpu.VMEM((PAIR, TERMS * SLAB, LANES), bf),
            pltpu.VMEM((2, BOND, 256), bf),
            pltpu.VMEM((BOND, BOND), f32),
            pltpu.VMEM((BOND, BOND), f32),
            pltpu.VMEM((BOND, BOND), f32),
            pltpu.VMEM((2, DEVS, 8, 128), f32),
            dma((2,)), dma, dma((CHUNKS, 3, 3)), dma((CHUNKS, 3, 3)), dma((CHUNKS, 10)), dma((CHUNKS, 10)),
            dma((2, DEVS)), dma((2, DEVS)),
        ],
        compiler_params=pltpu.CompilerParams(collective_id=0, has_side_effects=True, vmem_limit_bytes=67043328),
    )(psi_slab, rc, wi, left_all)


def slab_rows(arr):
    lead = arr.shape[:-3]
    parts = []
    for lo, hi in ((0, 16), (16, 32), (32, 40)):
        parts.append(arr[..., :, lo:hi, :].reshape(lead + (PAIR * (hi - lo), arr.shape[-1])))
    return jnp.concatenate(parts, axis=-2)


def slab_unrows(arr):
    lead = arr.shape[:-2]
    last = arr.shape[-1]
    parts = []
    for row, size in ((0, 16), (256, 16), (512, 8)):
        parts.append(arr[..., row:row + PAIR * size, :].reshape(lead + (PAIR, size, last)))
    return jnp.concatenate(parts, axis=-2)


def solution(mesh):
    def device_body(wavefunction, left_loc, pair_loc, right_loc, flag_loc):
        me = lax.axis_index(AXIS_NAME)
        left_all = lax.all_gather(left_loc, AXIS_NAME, axis=0, tiled=True)
        pair_all = lax.all_gather(pair_loc, AXIS_NAME, axis=0, tiled=True)
        flags = lax.all_gather(flag_loc, AXIS_NAME, axis=0, tiled=True)
        right_slab = lax.all_to_all(right_loc, AXIS_NAME, split_axis=1, concat_axis=0, tiled=True)
        cols = me * SLAB + jnp.arange(SLAB)
        ident = (cols[:, None] == jnp.arange(BOND)[None, :]).astype(bf)
        right_slab = jnp.where(flags[:, None, None] == 1, right_slab, ident[None])
        by_src = right_slab.reshape(TERMS, SLAB, DEVS, SLAB)
        main = by_src[..., :32].reshape(TERMS, SLAB, 512)
        tail = by_src[..., 32:]
        zero = jnp.zeros_like(tail)
        even = jnp.concatenate([tail, zero], axis=-1).reshape(TERMS, SLAB, 256)
        odd = jnp.concatenate([zero, tail], axis=-1).reshape(TERMS, SLAB, 256)
        cat = jnp.concatenate([main, even, odd], axis=-1).reshape(TERMS // 2, 2, SLAB, 1024)
        rc = jnp.concatenate([cat[:, 0], cat[:, 1, 32:], cat[:, 1, :32]], axis=1).reshape(TERMS * SLAB, 1024)
        eye = jnp.eye(16, dtype=bf)
        expand = (pair_all[:, :, None, :, None] * eye[None, None, :, None, :]).reshape(TERMS // 2, 2, 256, 256)
        low = (jnp.arange(256) % 16 < 8)[None, :, None]
        wi = jnp.stack([expand[:, 0], jnp.where(low, expand[:, 0], expand[:, 1]), expand[:, 1]], axis=1)
        psi_slab = lax.dynamic_slice_in_dim(wavefunction, me * SLAB, SLAB, axis=2)
        psi_slab = slab_rows(psi_slab.transpose(1, 2, 0))
        vecs, alphas, betas = run_lanczos(psi_slab, rc, wi, left_all)
        norm = betas[0, LANCZOS_STEPS]
        first = lax.dynamic_slice_in_dim(wavefunction, me * SLAB, SLAB, axis=0) / norm
        vecs = slab_unrows(vecs)
        vecs = lax.all_to_all(vecs, AXIS_NAME, split_axis=3, concat_axis=2, tiled=True)
        vecs = vecs.transpose(0, 3, 1, 2)
        krylov = jnp.concatenate([first[None], vecs], axis=0)
        return krylov, alphas[0, :LANCZOS_STEPS], betas[0, :LANCZOS_STEPS]

    return jax.shard_map(device_body, mesh=mesh, in_specs=(P(), P(AXIS_NAME), P(AXIS_NAME), P(AXIS_NAME), P(AXIS_NAME)), out_specs=(P(None, AXIS_NAME), P(), P()), check_vma=False)
```

time: 3730 us -> 1180 us (0.32)
  waiting for transfers between devices: 2170 us -> 122 us
  Pallas kernels: 0 us -> 535 us
  matrix products: 483 us -> 0 us
  blocking collectives: 382 us -> 73.4 us
  local copies, waits for them, and re-layouts: 560 us -> 280 us
  other arithmetic: 88.7 us -> 134 us
    reduce_scatter x6 -> x0, waiting for transfers between devices: 1850 us -> none  [device_body(): lax.psum_scatter(part_sigma, AXIS_NAME, scatter_dimension=0, tiled=True)]
    pallas_call x0 -> x1, Pallas kernels: none -> 535 us  [run_lanczos(): pl.pallas_call(lanczos_kernel, out_shape=(jax.ShapeDtypeStruct((LANCZOS_S...]
    dot_general x24 -> x0, matrix products: 483 us -> none  [the longest x12 327 us: term_body(): lax.dot_general(left_loc[term_idx], pair_done, (((1,), (1,)), ((), ())),...]
    psum x12 -> x0, blocking collectives: 382 us -> none  [the longest x6 196 us: device_body(): lax.psum(jnp.sum(residual * residual), AXIS_NAME) / vec_size]
    all_gather x5 -> x1, waiting for transfers between devices: 325 us -> 0.01 us  [device_body(): left_all = lax.all_gather(left_loc, AXIS_NAME, axis=0, tiled=True)]
    cond x12 -> x0, local copies, waits for them, and re-layouts: 279 us -> none  [term_body(): lax.cond(flag_loc[term_idx] == 1, apply_right, keep_vector, right_loc[ter...]
    while x6 -> x0, local copies, waits for them, and re-layouts: 197 us -> none  [local_sigma(): return lax.fori_loop(0, left_loc.shape[0], term_body, start_sum)]
    all_to_all x0 -> x2, waiting for transfers between devices: none -> 121 us  [the longest x1 121 us: device_body(): lax.all_to_all(vecs, AXIS_NAME, split_axis=3, concat_axis=2, tiled=True)]
  transfers between devices with their start and end apart: 11 -> 3, of which waited for: 11 -> 1; matrix products, arithmetic and copies ran while one was open for 0% -> 10% of each run, Pallas kernels for 0% -> 0%
where the time goes in v1:
time: 1180 us; the launch traced here: 1170 us
  Pallas kernels  535 us (45%)
  local copies, waits for them, and re-layouts  280 us (24%)
  other arithmetic  134 us (11%)
  waiting for transfers between devices  122 us (10%)
  blocking collectives  73.4 us (6%)
  between operations  14.7 us (1%)
    pallas_call x1, Pallas kernels, run_lanczos(): pl.pallas_call(lanczos_kernel, out_shape=(jax.ShapeDtypeStruct((LANCZOS_S...  535 us
    all_to_all x1, waiting for transfers between devices, device_body(): lax.all_to_all(vecs, AXIS_NAME, split_axis=3, concat_axis=2, tiled=True)  121 us
    all_to_all x1, other arithmetic, device_body(): lax.all_to_all(vecs, AXIS_NAME, split_axis=3, concat_axis=2, tiled=True)  105 us
    unnamed x16, local copies, waits for them, and re-layouts  86.9 us
    unnamed x1, blocking collectives  59.3 us
    all_to_all x3, local copies, waits for them, and re-layouts, device_body(): lax.all_to_all(vecs, AXIS_NAME, split_axis=3, concat_axis=2, tiled=True)  56.9 us
    mul x4, local copies, waits for them, and re-layouts, device_body(): pair_all[:, :, None, :, None] * eye[None, None, :, None, :]  52.3 us
    concatenate x1, local copies, waits for them, and re-layouts, slab_unrows(): return jnp.concatenate(parts, axis=-2)  25.5 us
  transfers between devices with their start and end apart: 3, of which 1 were waited for; matrix products, arithmetic and copies ran while one was open for 10% of the time, Pallas kernels for 0%

profile of v1, /device:TPU:0, one launch (start us, length us, event | category | flops | bytes accessed | tf_op | source)
XLA Modules:
  0.0 1167.4 jit_solution(4333941918395050930)
XLA Ops:
  7.2 0.0 copy-start.4
  7.2 0.0 all-gather.2.cloned.1.call-start
  7.2 0.7 all-gather.2.cloned.1.call-update
  7.9 4.3 copy.37
  12.2 0.0 copy-done.4
  12.2 0.2 dynamic-update-slice
  12.4 5.3 all-to-all-start
  17.7 59.3 %all-reduce.2 = s32[32]{0:T(128)S(1)} all-reduce(s32[32]{0:T(128)S(1)} %dynamic-update-slice), channel_id=1, replica_groups=mesh['terms'=16] {'terms'}, use_global_device_ids=true, to_apply=%add.2 | all-reduce | flops 32 | bytes 256
  77.0 5.6 dynamic-slice_bitcast_fusion
  82.6 3.8 slice.68
  86.4 5.6 fusion.3
  92.0 3.2 copy.34
  95.3 3.2 copy.35
  98.5 0.0 copy-start.1
  98.5 3.2 copy.36
  101.8 1.3 pad_maximum_fusion.5.psi_hbm
  103.1 0.0 copy-done.1
  103.2 14.1 %all_gather.10 = bf16[32,16,16]{2,1,0:T(8,128)(2,1)S(1)} all-gather(bf16[2,16,16]{2,1,0:T(8,128)(2,1)S(1)} %copy-done.1), channel_id=1, replica_groups=mesh['terms'=16] {'terms'}, dimensions={0}, use_global_device_ids=true | all-gather | bytes 17408 | tf_op jit(solution)/shard_map/all_gather | solution.py:313
  117.3 11.4 mul.26
  128.7 39.7 %mul.27 = bf16[16,2,256,256]{3,2,1,0:T(8,128)(2,1)} reshape(bf16[32,16,16,16,16]{4,3,2,1,0:T(8,128)(2,1)} %mul.26) | data formatting | bytes 8388608 | tf_op jit(solution)/shard_map/mul | solution.py:328
  168.4 0.2 mul.28
  168.6 1.0 mul.29
  169.6 0.1 compare_convert_fusion
  169.7 2.5 broadcast_multiply_fusion
  172.2 0.4 fusion.4
  172.6 3.1 pad_maximum_fusion.2.wi
  175.8 0.0 all-to-all-done
  175.8 0.2 copy.48
  176.0 8.6 all_to_all.29
  184.6 3.0 broadcast_select_fusion
  187.5 0.0 copy-start
  187.5 2.3 copy-done
  189.8 3.9 slice.70
  193.7 5.4 copy.45
  199.1 3.0 fusion.5
  202.1 1.9 copy.41
  204.0 1.9 copy.42
  205.9 7.2 concatenate.29
  213.1 0.1 maximum_bitcast_fusion
  213.2 0.4 pad_maximum_fusion.3
  213.6 0.1 slice_bitcast_fusion.1
  213.7 1.8 pad_maximum_fusion.4
  215.5 0.0 all-gather.2.cloned.1.call-done.left_hbm
  215.5 534.6 %shard_map.76 = (f32[6,640,640]{2,1,0:T(8,128)}, f32[1,8]{1,0:T(1,128)}, f32[1,8]{1,0:T(1,128)}) custom-call(f32[640,640]{1,0:T(8,128)} %pad_maximum_fusion.5.psi_hbm, bf16[1280,1024]{1,0:T(8,128)(2,1)} %bitcast.54, bf16[16,3,256,256]{3,2,1,0:T(8,128)(2,1)} %pad_maximum_fusion.2.wi, bf16[32,640,640]{2,1,0:T(8,128)(2,1)} %all-gather.2.cloned.1.call-done.left_hbm), custom_call_target="tpu_custom_call" | custom-call | tf_op jit(solution)/shard_map/pallas_call | solution.py:271
  750.1 3.8 fusion.2
  754.0 1.7 slice_bitcast_fusion
  755.7 4.6 pad_maximum_fusion.1
  760.3 25.5 %copy.43 = f32[6,16,40,640]{2,1,0,3:T(8,128)} copy(f32[6,16,40,640]{3,2,1,0:T(8,128)} %pad_maximum_fusion.1) | data formatting | bytes 19660800 | tf_op jit(solution)/shard_map/concatenate | solution.py:306
  785.8 33.8 %reshape.98 = f32[16,1,153600]{2,1,0:T(1,128)} reshape(f32[640,6,16,40]{3,2,1,0:T(8,128)} %bitcast.48) | data formatting | bytes 19660800
  819.6 0.0 copy-start.3
  819.6 0.0 copy-start.2
  819.6 3.7 all-to-all-start.1
  823.3 0.0 copy-done.3
  823.3 0.6 slice.60
  823.9 2.2 divide_bitcast_fusion
  826.1 0.0 copy-done.2
  826.1 0.5 slice_bitcast_fusion.2
  826.6 121.5 %all-to-all-done.1 = f32[16,1,153600]{2,1,0:T(1,128)} async-done(((f32[16,1,153600]{2,1,0:T(1,128)}), f32[16,1,153600]{2,1,0:T(1,128)}, u32[]{:S(2)}, u32[]{:S(2)}) %all-to-all-start.1) | async-done | bytes 9830432 | tf_op jit(solution)/shard_map/all_to_all | solution.py:337
  948.1 0.6 broadcast.56
  948.7 105.1 %reduce = f32[16,153600]{1,0:T(8,128)} reduce(f32[16,1,153600]{2,1,0:T(1,128)} %all-to-all-done.1, f32[]{:T(128)} %broadcast.56), dimensions={1}, to_apply=%all_to_all.30.reduce_sub_computation | reduce | bytes 19660804 | tf_op jit(solution)/shard_map/all_to_all | solution.py:337
  1053.7 41.0 %reshape.99 = f32[640,6,16,40]{3,2,1,0:T(8,128)} reshape(f32[16,153600]{1,0:T(8,128)} %reduce) | data formatting | bytes 19660800
  1094.7 30.6 %copy.44 = f32[6,16,16,40,40]{3,2,1,4,0:T(8,128)} copy(f32[6,16,16,40,40]{3,1,0,4,2:T(8,128)} %bitcast.49) | data formatting | bytes 19660800 | tf_op jit(solution)/shard_map/all_to_all | solution.py:337
  1125.3 25.7 %all_to_all.33 = f32[6,16,640,40]{2,1,3,0:T(8,128)} reshape(f32[6,16,16,40,40]{3,2,1,4,0:T(8,128)} %copy.44) | data formatting | bytes 19660800 | tf_op jit(solution)/shard_map/all_to_all | solution.py:337
  1151.0 9.1 pad_maximum_fusion
  (7 shorter events, 0.0 us)
Async XLA Ops:
  7.2 5.0 copy-start.4
  7.2 208.3 %all-gather.2.cloned.1.call-start = ((), (), s32[]{:S(2)}) async-start(), calls=%async_computation.2 | async-start | bytes 27852800 | tf_op jit(solution)/shard_map/all_gather | solution.py:312
  12.4 163.4 %all-to-all-start = ((bf16[2,640,640]{2,0,1:T(2,128)(2,1)}), bf16[2,640,640]{2,0,1:T(2,128)(2,1)S(1)}, u32[]{:S(2)}, u32[]{:S(2)}) async-start(bf16[2,640,640]{2,0,1:T(2,128)(2,1)} %copy.37), calls=%async_computation | async-start | bytes 3276800 | tf_op jit(solution)/shard_map/all_to_all | solution.py:315
  98.5 4.6 copy-start.1
  187.5 2.3 copy-start
  819.6 3.7 copy-start.3
  819.6 6.5 copy-start.2
  819.6 128.5 %all-to-all-start.1 = ((f32[16,1,153600]{2,1,0:T(1,128)}), f32[16,1,153600]{2,1,0:T(1,128)}, u32[]{:S(2)}, u32[]{:S(2)}) async-start(f32[16,1,153600]{2,1,0:T(1,128)} %reshape.98), calls=%async_computation.1 | async-start | bytes 19660800 | tf_op jit(solution)/shard_map/all_to_all | solution.py:337
Sparse Core Ops, SparseCore 0:
  10.2 127.2 all-gather.1

commit v2 on v0

v2 whole, which is shorter than its diff:
```python
import functools
import jax
import jax.numpy as jnp
from jax import lax
from jax.experimental import pallas as pl
from jax.sharding import PartitionSpec as P
from jax.experimental.pallas import tpu as pltpu

LANCZOS_STEPS = 6
AXIS_NAME = 'terms'
BOND = 640
PAIR = 16
TERMS = 32
DEVS = 16
SLAB = BOND // DEVS
CHUNKS = 5
LANES = 128
VEC_SIZE = BOND * PAIR * BOND
bf = jnp.bfloat16
f32 = jnp.float32
MESH = pl.DeviceIdType.MESH
PART_PAIRS = ((0, 3), (3, 6), (6, 8))
LEFT_ROWS = (((0, 48), (48, 96), (96, 128)), ((0, 32), (32, 80), (80, 128)), ((0, 48), (48, 80), (80, 128)))
D2D_FLIPS = ((0,), (1,), (2,), (0, 1), (0, 2), (1, 2), (0, 1, 2), ())
PART_AXES = ((0, 1, 2), (1, 2, 0), (2, 0, 1))


def lanczos_kernel(flags, psi, psi_rows, left_hbm, pair_hbm, right_hbm, gathered, alphas, betas,
                   u, lft, y, acc, cur, prev, ar, rc, wi, ops,
                   load_sem, stage_sem, own_sem, ici_send, ici_recv, d2d_send, d2d_recv, ar_send, ar_recv, out_send, out_recv, op_send, op_recv):
    me = lax.axis_index(AXIS_NAME)
    core = lax.rem(me, 2)
    place = (lax.rem(me // 2, 2), lax.rem(me // 4, 2), me // 8)
    across = tuple(me + (2 << n) * (1 - 2 * place[n]) for n in range(3))
    partner = me + 1 - 2 * core

    def slots(flips):
        return tuple(1 - place[n] if n in flips else place[n] for n in (2, 1, 0)) + (core,)

    def vec_view(ch, part, flips):
        pairs = PART_PAIRS[part] if part < 3 else (0, 8)
        return u.at[(ch, slice(pairs[0], pairs[1])) + slots(flips)]

    def left_view(ch, part, flips):
        lo, hi = LEFT_ROWS[ch % 3][part] if part < 3 else (0, 128)
        return lft.at[slots(flips) + (slice(None), slice(128 * ch + lo, 128 * ch + hi), slice(128 * ch, BOND))]

    def remote(ref, dst_ref, send, recv, dev):
        return pltpu.make_async_remote_copy(src_ref=ref, dst_ref=dst_ref, send_sem=send, recv_sem=recv, device_id=(dev,), device_id_type=MESH)

    def unit(view, ch, part, n, arriving=False):
        first, second, third = PART_AXES[part]
        flips, axis = (((), first), ((), second), ((), third), ((first,), second), ((first,), third), ((second,), third), ((first, second), third))[n]
        ref = view(ch, part, flips + (axis,) if arriving else flips)
        return remote(ref, ref, ici_send.at[ch, part, n], ici_recv.at[ch, part, n], across[axis])

    def start_units(view, ch, *which):
        for n in which:
            for part in range(3):
                unit(view, ch, part, n).start()

    def wait_units(view, ch, *which):
        for n in which:
            for part in range(3):
                unit(view, ch, part, n, True).wait_recv()

    def d2d(view, ch, n):
        ref = view(ch, 3, D2D_FLIPS[n])
        return remote(ref, ref, d2d_send.at[ch, n], d2d_recv.at[ch, n], partner)

    def own_out(view, ch):
        start_units(view, ch, 0, 1, 2)
        d2d(view, ch, 7).start()

    def relay_first(view, ch):
        for part in range(3):
            unit(view, ch, part, 0, True).wait_recv()
            unit(view, ch, part, 3).start()
        start_units(view, ch, 4)

    def relay_second(view, ch):
        for part in range(3):
            unit(view, ch, part, 1, True).wait_recv()
            unit(view, ch, part, 5).start()

    def relay_third(view, ch):
        wait_units(view, ch, 2)
        for n in (0, 1, 2):
            d2d(view, ch, n).start()

    def relay_last(view, ch):
        for part in range(3):
            unit(view, ch, part, 3, True).wait_recv()
            unit(view, ch, part, 6).start()

    def take_pairs(view, ch):
        wait_units(view, ch, 4, 5)
        for n in (3, 4, 5):
            d2d(view, ch, n).start()

    def take_last(view, ch):
        wait_units(view, ch, 6)
        d2d(view, ch, 6).start()

    def chunk_ready(view, ch):
        for n in range(8):
            d2d(view, ch, n).wait_recv()

    def drain_sends(view, ch):
        for n in range(8):
            d2d(view, ch, n).wait_send()
        for n in range(7):
            for part in range(3):
                unit(view, ch, part, n).wait_send()

    def for_left(ch, what):
        for c in range(CHUNKS):
            @pl.when(ch == c)
            def _():
                what(left_view, c)

    def send_partial(which, partial):
        ar[which, me] = partial
        for off in range(1, DEVS):
            dev = lax.rem(me + off, DEVS)
            ref = ar.at[which, me]
            remote(ref, ref, ar_send.at[which, off], ar_recv.at[which, me], dev).start()

    def total_of(which):
        for off in range(1, DEVS):
            dev = lax.rem(me + off, DEVS)
            ref = ar.at[which, dev]
            remote(ref, ref, ar_send.at[which, off], ar_recv.at[which, dev], dev).wait_recv()
        total = jnp.sum(jnp.sum(ar[which], axis=0))
        for off in range(1, DEVS):
            dev = lax.rem(me + off, DEVS)
            ref = ar.at[which, me]
            remote(ref, ref, ar_send.at[which, off], ar_recv.at[which, me], dev).wait_send()
        return total

    def all_sum(which, partial):
        send_partial(which, partial)
        return total_of(which)

    def dot_rows(fn):
        def body(g, tot):
            rows = pl.ds(pl.multiple_of(g * 16, 16), 16)
            val = fn(rows)
            for r in range(2):
                for c in range(5):
                    tot = tot + val[8 * r:8 * r + 8, 128 * c:128 * c + 128]
            return tot
        return lax.fori_loop(0, 40, body, jnp.zeros((8, 128), f32))

    def write_u():
        for ch in range(CHUNKS):
            lanes = slice(128 * ch, 128 * ch + 128)
            for i in range(8):
                dst = u.at[ch, i, place[2], place[1], place[0], core]
                dst[0:16] = cur[32 * i:32 * i + 16, lanes].astype(bf)
                dst[16:32] = cur[256 + 32 * i:256 + 32 * i + 16, lanes].astype(bf)
                dst[32:48] = cur[32 * i + 16:32 * i + 32, lanes].astype(bf)
                dst[48:64] = cur[256 + 32 * i + 16:256 + 32 * i + 32, lanes].astype(bf)
                dst[64:80] = cur[512 + 16 * i:512 + 16 * i + 16, lanes].astype(bf)

    def right_phase(ch, middle):
        for par in range(2):
            if par == 1:
                middle()
            rhs = []
            for i in range(8):
                main = u[ch, i, :, :, :, :, 32 * par:32 * par + 32, :].reshape(512, 128)
                tail = u[ch, i, :, :, :, :, 64:80, :].reshape(256, 128)
                rhs.append(jnp.concatenate([main, tail], axis=0))
            rhs = jnp.concatenate(rhs, axis=1)
            lhs = jnp.concatenate([rc[:, 0:512], rc[:, 512 + 256 * par:768 + 256 * par]], axis=1)
            val = jnp.dot(lhs, rhs, preferred_element_type=f32).astype(bf)
            for i in range(8):
                y[2 * i + par] = val[:, 128 * i:128 * i + 128]

    def pair_left_phase(ch, zb, half_done):
        low_rows = (iota((256, 256), 0) & 15) < 8

        @pl.loop(0, 2)
        def _(g):
            for s in range(8):
                k = g * 8 + s
                row = pl.multiple_of(k * 80, 16)
                tile = [y[:, pl.ds(row + 16 * t, 16), :].reshape(256, 128) for t in range(5)]
                z01 = jnp.dot(wi[k, 0], jnp.concatenate([tile[0], tile[1]], axis=1), preferred_element_type=f32).astype(bf)
                mixed = jnp.where(low_rows, wi[k, 0], wi[k, 1])
                z2 = jnp.dot(mixed, tile[2], preferred_element_type=f32).reshape(16, 2, 8, 128)
                z34 = jnp.dot(wi[k, 1], jnp.concatenate([tile[3], tile[4]], axis=1), preferred_element_type=f32).astype(bf)
                zb[s, 0:256, 0:128] = z01[:, 0:128]
                zb[s, 256:512, 0:128] = z01[:, 128:256]
                zb[s, 512:640, 0:128] = z2[:, 0].reshape(128, 128).astype(bf)
                zb[s, 0:256, 128:256] = z34[:, 0:128]
                zb[s, 256:512, 128:256] = z34[:, 128:256]
                zb[s, 512:640, 128:256] = z2[:, 1].reshape(128, 128).astype(bf)
            lhs = jnp.concatenate([zb[s] for s in range(8)], axis=1)
            rows = pl.ds(pl.multiple_of(ch * 128, 128), 128)
            rhs = jnp.concatenate([lft[g, s // 4, s // 2 % 2, s % 2, t, rows, :] for s in range(8) for t in range(2)], axis=0)
            acc[...] += jnp.dot(lhs, rhs, preferred_element_type=f32)

            @pl.when(g == 0)
            def _():
                half_done()

    def turn(turned):
        for lt in range(5):
            rows = []
            for n in range(16 * lt, 16 * lt + 16):
                q, part = n // 5, n % 5
                start = 512 + 8 * q if part == 4 else 256 * (part // 2) + 16 * q + 8 * (part % 2)
                rows.append(cur[start:start + 8, :])
            turned[:, 128 * lt:128 * lt + 128] = jnp.concatenate(rows, axis=0).T

    def flipped(mask):
        dev = me
        for n, bit in enumerate((core,) + place):
            if mask >> n & 1:
                dev = dev + (1 << n) * (1 - 2 * bit)
        return dev

    def out_copy(turned, vec, mask, arriving=False):
        dev = flipped(mask)
        src = dev if arriving else me
        rows = pl.ds(pl.multiple_of(dev * SLAB, 8), SLAB)
        return remote(turned.at[rows], gathered.at[vec, src], out_send.at[mask], out_recv.at[mask], dev)

    def own_copy(turned, vec):
        rows = pl.ds(pl.multiple_of(me * SLAB, 8), SLAB)
        return pltpu.make_async_copy(turned.at[rows], gathered.at[vec, me], own_sem)

    def send_out(turned, vec, masks):
        for mask in masks:
            out_copy(turned, vec, mask).start()

    def finish_out(turned, vec):
        own_copy(turned, vec).wait()
        for mask in range(1, DEVS):
            out_copy(turned, vec, mask, True).wait_recv()
        for mask in range(1, DEVS):
            out_copy(turned, vec, mask).wait_send()

    def iota(shape, dim):
        return lax.broadcasted_iota(jnp.int32, shape, dim)

    def op_copy(which, src_ref, dst_ref, off, dev, src):
        return remote(src_ref, dst_ref, op_send.at[which, off], op_recv.at[which, src], dev)

    def pair_copy(off, dev, src):
        return op_copy(0, ops.at[src], ops.at[src], off, dev, src)

    def right_copy(off, dev, src):
        rows = pl.ds(pl.multiple_of(dev * 80, 16), 80)
        into = pl.ds(pl.multiple_of(src * 80, 16), 80)
        return op_copy(1, y.at[5:10, rows], y.at[10:15, into], off, dev, src)

    def spread_right():
        col = iota((BOND, 128), 0)
        source = (col * 1639) >> 16
        within = col - source * SLAB
        target = jnp.where(within < 32, source * 32 + within, 480 + source * 8 + within)
        for t in range(5):
            perm = (target == iota((BOND, 128), 1) + 128 * t).astype(f32)
            for k in range(2):
                rows = jnp.concatenate([y[n, BOND * k:BOND * k + BOND, :] for n in range(5)], axis=1)
                val = jnp.dot(rows, perm.astype(bf), preferred_element_type=f32)
                val = jnp.where(flags[k] == 1, val, perm)
                val = val.reshape(DEVS, SLAB, 128)
                if k == 0:
                    first = val
            both_terms = jnp.concatenate([first, val[:, 32:], val[:, :32]], axis=1)
            y[5 + t] = both_terms.reshape(2 * BOND, 128).astype(bf)

    def build_right():
        rc[:, 0:512] = jnp.concatenate([y[10 + n] for n in range(4)], axis=1)
        src = iota((128, 256), 0)
        spot = 16 * (src >> 3) + (src & 7)
        for par in range(2):
            widen = (spot + 8 * par == iota((128, 256), 1)).astype(bf)
            rc[:, 512 + 256 * par:768 + 256 * par] = jnp.dot(y[14], widen, preferred_element_type=f32).astype(bf)

    def build_pairs():
        widen = ((iota((128, 256), 1) >> 4) == iota((128, 256), 0)).astype(bf)
        same = (iota((256, 256), 0) & 15) == (iota((256, 256), 1) & 15)

        @pl.loop(0, DEVS)
        def _(k):
            wide = []
            for t in range(2):
                tall = jnp.broadcast_to(ops[k, t].astype(f32)[:, None, :], (16, 16, 128)).reshape(256, 128).astype(bf)
                wide.append(jnp.where(same, jnp.dot(tall, widen, preferred_element_type=f32), 0.0))
            wi[k, 0] = wide[0].astype(bf)
            wi[k, 1] = wide[1].astype(bf)

    def tile_load(stage, t, ch, half):
        rows, qs = pl.ds(pl.multiple_of(128 * ch, 128), 128), pl.ds(pl.multiple_of(8 * half, 8), 8)
        return pltpu.make_async_copy(psi.at[rows, qs, 128 * t:128 * t + 128], stage.at[t], stage_sem.at[t])

    def start_vector(norm, stage, flip):
        base = (me * SLAB) // 128
        skip = pl.multiple_of(me * SLAB - base * 128, 8)
        for t in range(5):
            tile_load(stage, t, 0, 0).start()

        @pl.loop(0, 2 * CHUNKS)
        def _(it):
            ch, half = it // 2, lax.rem(it, 2)
            for t in range(5):
                tile_load(stage, t, ch, half).wait()
            lanes = pl.ds(pl.multiple_of(128 * ch, 128), 128)

            @pl.when(it == 4)
            def _():
                relay_first(left_view, 0)
                relay_second(left_view, 0)
                relay_third(left_view, 0)

            for q in range(8):
                for t in range(2):
                    flip[q, 128 * t:128 * t + 128, :] = stage[jnp.minimum(base + t, 4), :, q, :].T
                val = flip[q, pl.ds(skip, SLAB), :] / norm
                row = 128 * half + 16 * q
                for start, piece, size in ((row, 0, 16), (256 + row, 16, 16), (512 + 64 * half + 8 * q, 32, 8)):
                    cur[pl.ds(pl.multiple_of(start, 8), size), lanes] = val[piece:piece + size, :]
            for t in range(5):
                for q in range(8):
                    val = (stage[t, :, q, :].T / norm).astype(bf)
                    for m in range(16):
                        src, piece = (16 * t + m) // 5, (16 * t + m) % 5
                        row = 64 + 8 * (q % 2) if piece == 4 else 32 * (q % 2) + 8 * piece
                        u[ch, 4 * half + q // 2, src // 8, src // 4 % 2, src // 2 % 2, src % 2, row:row + 8, :] = val[8 * m:8 * m + 8, :]

                @pl.when(it + 1 < 2 * CHUNKS)
                def _():
                    tile_load(stage, t, (it + 1) // 2, lax.rem(it + 1, 2)).start()

    def mirror_left(ch):
        @pl.loop(0, 8)
        def _(g):
            for n in range(4):
                at = (g // 4, lax.rem(g // 2, 2), lax.rem(g, 2), n // 2, n % 2)
                for other in range(ch + 1, CHUNKS):
                    block = lft[at + (slice(128 * ch, 128 * ch + 128), slice(128 * other, 128 * other + 128))]
                    lft[at + (slice(128 * other, 128 * other + 128), slice(128 * ch, 128 * ch + 128))] = block.T

    left_load = pltpu.make_async_copy(left_hbm, lft.at[place[2], place[1], place[0], core], load_sem.at[0])
    slab_load = pltpu.make_async_copy(psi_rows.at[pl.ds(pl.multiple_of(me * BOND, 8), BOND)], cur, load_sem.at[1])
    pair_load = pltpu.make_async_copy(pair_hbm, ops.at[me], load_sem.at[2])
    right_load = [pltpu.make_async_copy(right_hbm.at[:, 128 * n:128 * n + 128], y.at[n], load_sem.at[3 + n]) for n in range(5)]
    pair_load.start()
    slab_load.start()
    for load in right_load:
        load.start()
    left_load.start()
    barrier = pltpu.get_barrier_semaphore()
    for off in range(1, DEVS):
        pl.semaphore_signal(barrier, inc=1, device_id=(lax.rem(me + off, DEVS),), device_id_type=MESH)
    pl.semaphore_wait(barrier, DEVS - 1)
    pair_load.wait()
    for off in range(1, DEVS):
        pair_copy(off, lax.rem(me + off, DEVS), me).start()
    slab_load.wait()
    send_partial(1, dot_rows(lambda rows: cur[rows, :] * cur[rows, :]))
    for load in right_load:
        load.wait()
    spread_right()
    left_load.wait()
    own_out(left_view, 0)
    for off in range(1, DEVS):
        right_copy(off, lax.rem(me + off, DEVS), me).start()
    own = pl.ds(pl.multiple_of(me * 80, 16), 80)
    y[10:15, own] = y[5:10, own]
    norm = jnp.sqrt(total_of(1) / VEC_SIZE)
    betas[0, LANCZOS_STEPS] = norm
    pl.run_scoped(functools.partial(start_vector, norm), pltpu.VMEM((5, 128, 8, LANES), f32), pltpu.VMEM((8, 256, LANES), f32))
    for off in range(1, DEVS):
        dev = lax.rem(me + off, DEVS)
        pair_copy(off, dev, dev).wait_recv()
    build_pairs()
    for off in range(1, DEVS):
        dev = lax.rem(me + off, DEVS)
        rows = pl.ds(pl.multiple_of(dev * 80, 16), 80)
        op_copy(1, y.at[5:10, rows], y.at[10:15, rows], off, dev, dev).wait_recv()
    build_right()
    relay_last(left_view, 0)
    own_out(left_view, 1)
    for off in range(1, DEVS):
        dev = lax.rem(me + off, DEVS)
        pair_copy(off, dev, me).wait_send()
        right_copy(off, dev, me).wait_send()
    prev[...] = jnp.zeros_like(prev)

    def step(zb, turned, j, beta_prev):
        acc[...] = jnp.zeros_like(acc)

        later = j > 0

        @pl.when(later)
        def _():
            own_out(vec_view, 0)
            turn(turned)
            own_copy(turned, j - 1).start()
            relay_first(vec_view, 0)
            relay_second(vec_view, 0)
            relay_last(vec_view, 0)
            own_out(vec_view, 1)
            relay_third(vec_view, 0)
            take_pairs(vec_view, 0)
            take_last(vec_view, 0)
            chunk_ready(vec_view, 0)

        @pl.loop(0, CHUNKS)
        def _(ch):
            @pl.when(later & (ch + 1 < CHUNKS))
            def _():
                relay_first(vec_view, ch + 1)

            def middle():
                @pl.when(later & (ch + 1 < CHUNKS))
                def _():
                    relay_second(vec_view, ch + 1)

            right_phase(ch, middle)

            @pl.when(later & (ch + 1 < CHUNKS))
            def _():
                relay_third(vec_view, ch + 1)
                relay_last(vec_view, ch + 1)

                @pl.when(ch + 2 < CHUNKS)
                def _():
                    own_out(vec_view, ch + 2)

                @pl.when(ch == 3)
                def _():
                    send_out(turned, j - 1, (1, 3, 5, 9, 14, 15))

            @pl.when(later & (ch == 4))
            def _():
                send_out(turned, j - 1, (7, 13, 11))

            @pl.when(j == 0)
            def _():
                def left_ready(view, c):
                    take_pairs(view, c)
                    take_last(view, c)
                    chunk_ready(view, c)
                    mirror_left(c)

                for_left(ch, left_ready)
                for_left(ch + 1, relay_first)

            def half_done():
                @pl.when(later & (ch + 1 < CHUNKS))
                def _():
                    take_pairs(vec_view, ch + 1)
                    take_last(vec_view, ch + 1)

                    @pl.when(ch == 2)
                    def _():
                        send_out(turned, j - 1, (2, 4, 8))

                    @pl.when(ch == 3)
                    def _():
                        send_out(turned, j - 1, (6, 12, 10))

                @pl.when(j == 0)
                def _():
                    for_left(ch + 1, relay_second)

            pair_left_phase(ch, zb, half_done)

            @pl.when(later & (ch + 1 < CHUNKS))
            def _():
                chunk_ready(vec_view, ch + 1)

            @pl.when(j == 0)
            def _():
                def advance(view, c):
                    relay_third(view, c)
                    relay_last(view, c)

                for_left(ch + 1, advance)
                for_left(ch + 2, own_out)

        @pl.loop(0, CHUNKS)
        def _(ch):
            @pl.when(j == 0)
            def _():
                for_left(ch, drain_sends)

            @pl.when(later)
            def _():
                drain_sends(vec_view, ch)

        @pl.when(later)
        def _():
            finish_out(turned, j - 1)

        alpha = all_sum(0, dot_rows(lambda rows: acc[rows, :] * cur[rows, :])) / VEC_SIZE

        def residual(rows):
            w = acc[rows, :] - alpha * cur[rows, :] - beta_prev * prev[rows, :]
            acc[rows, :] = w
            return w * w

        beta = jnp.sqrt(all_sum(1, dot_rows(residual)) / VEC_SIZE)
        alphas[0, j] = alpha
        betas[0, j] = beta

        @pl.loop(0, 40)
        def _(g):
            rows = pl.ds(pl.multiple_of(g * 16, 16), 16)
            prev[rows, :] = cur[rows, :]
            cur[rows, :] = acc[rows, :] / beta

        @pl.when(j + 1 < LANCZOS_STEPS)
        def _():
            write_u()

        return beta

    def all_steps(zb, turned):
        lax.fori_loop(0, LANCZOS_STEPS, functools.partial(step, zb, turned), jnp.zeros((), f32))
        turn(turned)
        own_copy(turned, LANCZOS_STEPS - 1).start()
        send_out(turned, LANCZOS_STEPS - 1, (14, 15, 6, 12, 10, 7, 13, 11, 2, 4, 8, 3, 5, 9, 1))
        finish_out(turned, LANCZOS_STEPS - 1)

    pl.run_scoped(all_steps, pltpu.VMEM((8, BOND, 256), bf), pltpu.VMEM((BOND, BOND), f32))


def run_lanczos(flags, psi, left_loc, pair_loc, right_loc):
    smem = pl.BlockSpec(memory_space=pltpu.SMEM)
    hbm = pl.BlockSpec(memory_space=pltpu.HBM)
    dma = pltpu.SemaphoreType.DMA
    return pl.pallas_call(
        lanczos_kernel,
        out_shape=(jax.ShapeDtypeStruct((LANCZOS_STEPS, DEVS, SLAB, BOND), f32), jax.ShapeDtypeStruct((1, 8), f32), jax.ShapeDtypeStruct((1, 8), f32)),
        in_specs=[smem, hbm, hbm, hbm, hbm, hbm],
        out_specs=(hbm, smem, smem),
        scratch_shapes=[
            pltpu.VMEM((CHUNKS, 8, 2, 2, 2, 2, 80, LANES), bf),
            pltpu.VMEM((2, 2, 2, 2, 2, BOND, BOND), bf),
            pltpu.VMEM((PAIR, TERMS * SLAB, LANES), bf),
            pltpu.VMEM((BOND, BOND), f32),
            pltpu.VMEM((BOND, BOND), f32),
            pltpu.VMEM((BOND, BOND), f32),
            pltpu.VMEM((2, DEVS, 8, 128), f32),
            pltpu.VMEM((TERMS * SLAB, 1024), bf),
            pltpu.VMEM((DEVS, 2, 256, 256), bf),
            pltpu.VMEM((DEVS, 2, PAIR, LANES), bf),
            dma((8,)), dma((5,)), dma, dma((CHUNKS, 3, 7)), dma((CHUNKS, 3, 7)), dma((CHUNKS, 8)), dma((CHUNKS, 8)),
            dma((2, DEVS)), dma((2, DEVS)), dma((DEVS,)), dma((DEVS,)), dma((2, DEVS)), dma((2, DEVS)),
        ],
        compiler_params=pltpu.CompilerParams(collective_id=0, has_side_effects=True, vmem_limit_bytes=67043328),
    )(flags, psi, psi.reshape(BOND * PAIR, BOND), left_loc, pair_loc, right_loc.reshape(2 * BOND, BOND))


def place_kernel(first_block, norm, psi, gathered, out):
    vec = pl.program_id(0)

    @pl.when(vec == 0)
    def _():
        out[0] = psi[...] / norm[0, LANCZOS_STEPS]

    @pl.when(vec > 0)
    def _():
        for r in range(0, SLAB, 8):
            for q in range(PAIR):
                out[0, r:r + 8, q, :] = jnp.concatenate([gathered[0, src, r:r + 8, SLAB * q:SLAB * q + SLAB] for src in range(DEVS)], axis=1)


def place_outputs(first_block, norm, wavefunction, gathered):
    return pl.pallas_call(
        place_kernel,
        out_shape=jax.ShapeDtypeStruct((LANCZOS_STEPS + 1, SLAB, PAIR, BOND), f32),
        grid_spec=pltpu.PrefetchScalarGridSpec(
            num_scalar_prefetch=1,
            grid=(LANCZOS_STEPS + 1,),
            in_specs=[
                pl.BlockSpec(memory_space=pltpu.SMEM),
                pl.BlockSpec((SLAB, PAIR, BOND), lambda v, first: (first[0], 0, 0)),
                pl.BlockSpec((1, DEVS, SLAB, BOND), lambda v, first: (jnp.maximum(v - 1, 0), 0, 0, 0)),
            ],
            out_specs=pl.BlockSpec((1, SLAB, PAIR, BOND), lambda v, first: (v, 0, 0, 0)),
        ),
    )(first_block, norm, wavefunction, gathered)


def solution(mesh):
    def device_body(wavefunction, left_loc, pair_loc, right_loc, flag_loc):
        me = lax.axis_index(AXIS_NAME)
        pair_pad = jnp.pad(pair_loc, ((0, 0), (0, 0), (0, LANES - PAIR)))
        vecs, alphas, betas = run_lanczos(flag_loc, wavefunction, left_loc, pair_pad, right_loc)
        krylov = place_outputs(me.reshape(1), betas, wavefunction, vecs)
        return krylov, alphas[0, :LANCZOS_STEPS], betas[0, :LANCZOS_STEPS]

    return jax.shard_map(device_body, mesh=mesh, in_specs=(P(), P(AXIS_NAME), P(AXIS_NAME), P(AXIS_NAME), P(AXIS_NAME)), out_specs=(P(None, AXIS_NAME), P(), P()), check_vma=False)
```

time: 3730 us -> 572 us (0.15)
  waiting for transfers between devices: 2170 us -> 0 us
  Pallas kernels: 0 us -> 569 us
  local copies, waits for them, and re-layouts: 560 us -> 1.83 us
  matrix products: 483 us -> 0 us
  blocking collectives: 382 us -> 0 us
  other arithmetic: 88.7 us -> 0 us
    reduce_scatter x6 -> x0, waiting for transfers between devices: 1850 us -> none  [device_body(): lax.psum_scatter(part_sigma, AXIS_NAME, scatter_dimension=0, tiled=True)]
    pallas_call x0 -> x2, Pallas kernels: none -> 569 us  [the longest x1 554 us: run_lanczos(): pl.pallas_call(lanczos_kernel, out_shape=(jax.ShapeDtypeStruct((LANCZOS_S...]
    dot_general x24 -> x0, matrix products: 483 us -> none  [the longest x12 327 us: term_body(): lax.dot_general(left_loc[term_idx], pair_done, (((1,), (1,)), ((), ())),...]
    psum x12 -> x0, blocking collectives: 382 us -> none  [the longest x6 196 us: device_body(): lax.psum(jnp.sum(residual * residual), AXIS_NAME) / vec_size]
    all_gather x5 -> x0, waiting for transfers between devices: 325 us -> none  [device_body(): lax.all_gather(following.astype(jnp.bfloat16), AXIS_NAME, axis=0, tiled=T...]
    cond x12 -> x0, local copies, waits for them, and re-layouts: 279 us -> none  [term_body(): lax.cond(flag_loc[term_idx] == 1, apply_right, keep_vector, right_loc[ter...]
    while x6 -> x0, local copies, waits for them, and re-layouts: 197 us -> none  [local_sigma(): return lax.fori_loop(0, left_loc.shape[0], term_body, start_sum)]
    unnamed x44 -> x4, local copies, waits for them, and re-layouts: 75.6 us -> 0.01 us
  transfers between devices with their start and end apart: 11 -> 0, of which waited for: 11 -> 0; matrix products, arithmetic and copies ran while one was open for 0% -> 0% of each run, Pallas kernels for 0% -> 0%
where the time goes in v2:
time: 572 us; the launch traced here: 571 us
  Pallas kernels  569 us (99%)
    pallas_call x1, Pallas kernels, run_lanczos(): pl.pallas_call(lanczos_kernel, out_shape=(jax.ShapeDtypeStruct((LANCZOS_S...  554 us
    pallas_call x1, Pallas kernels, place_outputs(): pl.pallas_call(place_kernel, out_shape=jax.ShapeDtypeStruct((LANCZOS_STEP...  14.9 us

profile of v2, /device:TPU:0, one launch (start us, length us, event | category | flops | bytes accessed | tf_op | source)
XLA Modules:
  0.0 571.1 jit_solution(6042682921657295141)
XLA Ops:
  0.6 1.3 pad.4.pair_hbm
  1.9 553.7 %shard_map.76 = (f32[6,16,40,640]{3,2,1,0:T(8,128)}, f32[1,8]{1,0:T(1,128)}, f32[1,8]{1,0:T(1,128)}) custom-call(s32[2]{0:T(128)} %flags.1, f32[640,16,640]{2,1,0:T(8,128)} %psi.3, f32[10240,640]{1,0:T(8,128)} %bitcast.7, bf16[2,640,640]{2,1,0:T(8,128)(2,1)} %left_hbm.1, bf16[2,16,128]{2,1,0:T(8,128)(2,1)} %pad.4.pair_hbm, bf16[1280,640]{1,0:T(8,128)(2,1)} %bitcast.8), custom_call_target="tpu_custom_call" | custom-call | tf_op jit(solution)/shard_map/pallas_call | solution.py:540
  555.6 0.0 copy-start
  555.6 0.0 copy-start.1
  555.6 14.9 %shard_map.77 = f32[7,40,16,640]{3,2,1,0:T(8,128)} custom-call(s32[1]{0:T(128)} %bitcast.first_block, f32[1,8]{1,0:T(1,128)} %get-tuple-element.6.norm, f32[640,16,640]{2,1,0:T(8,128)} %psi.3, f32[6,16,40,640]{3,2,1,0:T(8,128)} %get-tuple-element.7.gathered), custom_call_target="tpu_custom_call" | custom-call | tf_op jit(solution)/shard_map/pallas_call | solution.py:578
  570.6 0.0 copy-done
  570.6 0.0 copy-done.1
  570.6 0.5 slice_bitcast_fusion
Async XLA Ops:
  555.6 15.0 %copy-start = (f32[1,8]{1,0:T(1,128)S(1)}, f32[1,8]{1,0:T(1,128)}, u32[]{:S(2)}) copy-start(f32[1,8]{1,0:T(1,128)} %get-tuple-element.6.norm) | copy-start | bytes 100
  555.6 15.0 %copy-start.1 = (f32[1,8]{1,0:T(1,128)S(1)}, f32[1,8]{1,0:T(1,128)}, u32[]{:S(2)}) copy-start(f32[1,8]{1,0:T(1,128)} %get-tuple-element.8) | copy-start | bytes 100

commit v3 on v0

v3 whole, which is shorter than its diff:
```python
import functools
import jax
import jax.numpy as jnp
from jax import lax
from jax.experimental import pallas as pl
from jax.sharding import PartitionSpec as P
from jax.experimental.pallas import tpu as pltpu

LANCZOS_STEPS = 6
AXIS_NAME = 'terms'
BOND = 640
PAIR = 16
TERMS = 32
DEVS = 16
SLAB = BOND // DEVS
CHUNKS = 5
FEW = 20
LANES = 128
VEC_SIZE = BOND * PAIR * BOND
bf = jnp.bfloat16
f32 = jnp.float32
MESH = pl.DeviceIdType.MESH
PART_PAIRS = ((0, 3), (3, 6), (6, 8))
LEFT_ROWS = ((0, 48), (48, 96), (96, 128))
AXES = ((1, 0, 0), (0, 1, 0), (0, 0, 1))
D2D_FLIPS = ((0,), (1,), (2,), (0, 1), (0, 2), (1, 2), (0, 1, 2), ())


def entry_barrier(me):
    barrier = pltpu.get_barrier_semaphore()
    for off in range(1, DEVS):
        pl.semaphore_signal(barrier, inc=1, device_id=(lax.rem(me + off, DEVS),), device_id_type=MESH)
    pl.semaphore_wait(barrier, DEVS - 1)


def iota(shape, dim):
    return lax.broadcasted_iota(jnp.int32, shape, dim)


def remote(ref, dst_ref, send, recv, dev):
    return pltpu.make_async_remote_copy(src_ref=ref, dst_ref=dst_ref, send_sem=send, recv_sem=recv, device_id=(dev,), device_id_type=MESH)


class Spot:
    def __init__(self, net, ch):
        self.ch = ch
        self.hits, self.across = [], []
        for n in range(3):
            axis = (n + ch) % 3 if isinstance(ch, int) else lax.rem(n + ch, 3)
            one = axis * (2 - axis)
            two = axis * (axis - 1) // 2 if isinstance(ch, int) else lax.div(axis * (axis - 1), 2)
            hit = (1 - one - two, one, two)
            self.hits.append(hit)
            self.across.append(net.me + hit[0] * net.step[0] + hit[1] * net.step[1] + hit[2] * net.step[2])


class Gather:
    def __init__(self, me, ici_send, ici_recv, d2d_send, d2d_recv):
        self.me, self.sems = me, (ici_send, ici_recv, d2d_send, d2d_recv)
        self.core = lax.rem(me, 2)
        self.place = (lax.rem(lax.div(me, 2), 2), lax.rem(lax.div(me, 4), 2), lax.div(me, 8))
        self.turn = tuple(1 - 2 * at for at in self.place)
        self.step = tuple((2 << n) * turn for n, turn in enumerate(self.turn))
        self.partner = me + 1 - 2 * self.core

    def at(self, ch):
        return Spot(self, ch)

    def slots(self, hits):
        idx = []
        for n in (2, 1, 0):
            moved = self.place[n]
            for hit in hits:
                if not isinstance(hit[n], int) or hit[n]:
                    moved = moved + hit[n] * self.turn[n]
            idx.append(moved)
        return tuple(idx) + (self.core,)

    def unit(self, view, spot, part, n, arriving=False):
        flips, axis = (((), 0), ((), 1), ((), 2), ((0,), 1), ((0,), 2), ((1,), 2), ((0, 1), 2))[n]
        hits = [spot.hits[(part + m) % 3] for m in (flips + (axis,) if arriving else flips)]
        ref = view(spot.ch, part, hits)
        return remote(ref, ref, self.sems[0].at[spot.ch, part, n], self.sems[1].at[spot.ch, part, n], spot.across[(part + axis) % 3])

    def start_units(self, view, spot, *which):
        for n in which:
            for part in range(3):
                self.unit(view, spot, part, n).start()

    def wait_units(self, view, spot, *which):
        for n in which:
            for part in range(3):
                self.unit(view, spot, part, n, True).wait_recv()

    def d2d(self, view, spot, n):
        ref = view(spot.ch, 3, [AXES[m] for m in D2D_FLIPS[n]])
        return remote(ref, ref, self.sems[2].at[spot.ch, n], self.sems[3].at[spot.ch, n], self.partner)

    def own_out(self, view, spot):
        self.start_units(view, spot, 0, 1, 2)
        self.d2d(view, spot, 7).start()

    def relay_first(self, view, spot):
        for part in range(3):
            self.unit(view, spot, part, 0, True).wait_recv()
            self.unit(view, spot, part, 3).start()
        self.start_units(view, spot, 4)

    def relay_second(self, view, spot):
        for part in range(3):
            self.unit(view, spot, part, 1, True).wait_recv()
            self.unit(view, spot, part, 5).start()

    def relay_third(self, view, spot):
        self.wait_units(view, spot, 2)
        for n in (0, 1, 2):
            self.d2d(view, spot, n).start()

    def relay_last(self, view, spot):
        for part in range(3):
            self.unit(view, spot, part, 3, True).wait_recv()
            self.unit(view, spot, part, 6).start()

    def take_pairs(self, view, spot):
        self.wait_units(view, spot, 4, 5)
        for n in (3, 4, 5):
            self.d2d(view, spot, n).start()

    def take_last(self, view, spot):
        self.wait_units(view, spot, 6)
        self.d2d(view, spot, 6).start()

    def chunk_ready(self, view, spot):
        for n in range(8):
            self.d2d(view, spot, n).wait_recv()

    def drain_sends(self, view, spot):
        for n in range(8):
            self.d2d(view, spot, n).wait_send()
        for n in range(7):
            for part in range(3):
                self.unit(view, spot, part, n).wait_send()


def prep_kernel(flags, psi, psi_rows, pair_loc, right_hbm, left_hbm, table, few, norm_out, u_hbm, slab_hbm, wi_hbm, right_out, left_out,
                u, y, moved, cur, seen, ops, wi, left, load_sem, stage_sem, out_sem, seen_send, seen_recv, op_send, op_recv, ici_send, ici_recv, d2d_send, d2d_recv):
    me = lax.axis_index(AXIS_NAME)
    net = Gather(me, ici_send, ici_recv, d2d_send, d2d_recv)

    def left_view(ch, part, flips):
        lo, hi = LEFT_ROWS[part] if part < 3 else (0, 128)
        return left.at[net.slots(flips) + (slice(None), slice(lo, hi))]

    def dots(fn, count):
        def body(g, tots):
            rows = pl.ds(pl.multiple_of(g * 16, 16), 16)
            out = []
            for tot, val in zip(tots, fn(rows)):
                for r in range(2):
                    for c in range(5):
                        tot = tot + val[8 * r:8 * r + 8, 128 * c:128 * c + 128]
                out.append(tot)
            return tuple(out)
        return lax.fori_loop(0, 40, body, (jnp.zeros((8, LANES), f32),) * count)

    def spread_right():
        col = iota((BOND, 128), 0)
        source = (col * 1639) >> 16
        within = col - source * SLAB
        target = jnp.where(within < 32, source * 32 + within, 480 + source * 8 + within)
        for t in range(5):
            perm = (target == iota((BOND, 128), 1) + 128 * t).astype(f32).astype(bf)
            for k in range(2):
                rows = jnp.concatenate([y[n, BOND * k:BOND * k + BOND, :] for n in range(5)], axis=1)
                val = jnp.dot(rows, perm, preferred_element_type=f32).reshape(DEVS, SLAB, 128)
                if k == 0:
                    first = val
            moved[t] = jnp.concatenate([first[:, None], val[:, None]], axis=1).reshape(TERMS, SLAB, 128).astype(bf)

    def build_pairs():
        widen = ((iota((128, 256), 1) >> 4) == iota((128, 256), 0)).astype(bf)
        same = (iota((256, 256), 0) & 15) == (iota((256, 256), 1) & 15)

        @pl.loop(0, DEVS)
        def _(k):
            wide = []
            for t in range(2):
                tall = jnp.broadcast_to(ops[k, t].astype(f32)[:, None, :], (16, 16, 128)).reshape(256, 128).astype(bf)
                wide.append(jnp.where(same, jnp.dot(tall, widen, preferred_element_type=f32), 0.0))
            wi[k, 0] = wide[0].astype(bf)
            wi[k, 1] = wide[1].astype(bf)

    def tile_load(stage, t, ch, half):
        rows, qs = pl.ds(pl.multiple_of(128 * ch, 128), 128), pl.ds(pl.multiple_of(8 * half, 8), 8)
        return pltpu.make_async_copy(psi.at[rows, qs, 128 * t:128 * t + 128], stage.at[t], stage_sem.at[t])

    def vector_out(ch):
        return pltpu.make_async_copy(u.at[ch], u_hbm.at[ch], out_sem.at[ch])

    def start_vector(norm, stage, flip):
        base = (me * SLAB) // 128
        skip = pl.multiple_of(me * SLAB - base * 128, 8)
        for t in range(5):
            tile_load(stage, t, 0, 0).start()

        @pl.loop(0, 2 * CHUNKS)
        def _(it):
            ch, half = it // 2, lax.rem(it, 2)
            @pl.when(it == 3)
            def _():
                net.relay_first(left_view, net.at(0))

            @pl.when(it == 4)
            def _():
                net.relay_second(left_view, net.at(0))
                send_right(5, 10)

            @pl.when(it == 6)
            def _():
                net.relay_third(left_view, net.at(0))

            @pl.when(it == 8)
            def _():
                net.relay_last(left_view, net.at(0))
                send_right(10, 15)

            for t in range(5):
                tile_load(stage, t, ch, half).wait()

                @pl.when((base == t) | (base + 1 == t))
                def _():
                    rows = pl.ds(pl.multiple_of(128 * (t - base), 128), 128)
                    for q in range(8):
                        flip[q, rows, :] = stage[t, :, q, :].T

                for q in range(8):
                    val = (stage[t, :, q, :].T / norm).astype(bf)
                    for m in range(16):
                        src, piece = (16 * t + m) // 5, (16 * t + m) % 5
                        row = 64 + 8 * (q % 2) if piece == 4 else 32 * (q % 2) + 8 * piece
                        u[ch, 4 * half + q // 2, src // 8, src // 4 % 2, src // 2 % 2, src % 2, row:row + 8, :] = val[8 * m:8 * m + 8, :]

                @pl.when(it + 1 < 2 * CHUNKS)
                def _():
                    tile_load(stage, t, (it + 1) // 2, lax.rem(it + 1, 2)).start()

            lanes = pl.ds(pl.multiple_of(128 * ch, 128), 128)
            for q in range(8):
                val = flip[q, pl.ds(skip, SLAB), :] / norm
                row = 128 * half + 16 * q
                for start, piece, size in ((row, 0, 16), (256 + row, 16, 16), (512 + 64 * half + 8 * q, 32, 8)):
                    cur[pl.ds(pl.multiple_of(start, 8), size), lanes] = val[piece:piece + size, :]

            @pl.when(half == 1)
            def _():
                vector_out(ch).start()

    def seen_copy(off, dev, src):
        return remote(seen.at[src], seen.at[src], seen_send.at[off], seen_recv.at[src], dev)

    def pair_copy(off, dev, src):
        return remote(ops.at[src], ops.at[src], op_send.at[0, off], op_recv.at[0, src], dev)

    def right_copy(off, dev, src):
        return remote(moved.at[:, pl.ds(2 * dev, 2)], right_out.at[:, pl.ds(2 * src, 2)], op_send.at[1, off], op_recv.at[1, src], dev)

    def others():
        return [(off, lax.rem(me + off, DEVS)) for off in range(1, DEVS)]

    def send_right(first, last):
        for n in range(first, last):
            off = 3 * (n % 5) + n // 5 + 1
            right_copy(off, lax.rem(me + off, DEVS), me).start()

    slab_load = pltpu.make_async_copy(psi_rows.at[pl.ds(pl.multiple_of(me * BOND, 8), BOND)], cur, load_sem.at[0])
    left_load = pltpu.make_async_copy(left_hbm.at[:, 0:128], left.at[net.slots(())], load_sem.at[1])
    right_load = [pltpu.make_async_copy(right_hbm.at[:, 128 * n:128 * n + 128], y.at[n], load_sem.at[2 + n]) for n in range(5)]
    slab_load.start()
    left_load.start()
    for load in right_load:
        load.start()
    for t in range(2):
        ops[me, t] = jnp.concatenate([pair_loc[t].astype(f32), jnp.zeros((PAIR, LANES - PAIR), f32)], axis=1).astype(bf)
    entry_barrier(me)
    slab_load.wait()
    square, = dots(lambda rows: (cur[rows, :] * cur[rows, :],), 1)
    row = iota((8, LANES), 0)
    full = jnp.where(row == 1, flags[0], flags[1]).astype(f32)
    seen[me] = jnp.where(row == 0, jnp.sum(square, axis=0, keepdims=True), full)
    for off, dev in others():
        seen_copy(off, dev, me).start()
    for off, dev in others():
        pair_copy(off, dev, me).start()
    left_load.wait()
    net.own_out(left_view, net.at(0))
    for load in right_load:
        load.wait()
    spread_right()
    send_right(0, 5)
    own = pl.ds(2 * me, 2)
    right_own = pltpu.make_async_copy(moved.at[:, own], right_out.at[:, own], load_sem.at[0])
    right_own.start()
    for off, dev in others():
        seen_copy(off, dev, dev).wait_recv()
    norm = jnp.sqrt(jnp.sum(jnp.sum(seen[:, 0:1, :], axis=0)) / VEC_SIZE)
    norm_out[0] = norm
    term, lane = iota((TERMS, LANES), 0), iota((TERMS, LANES), 1)
    full = jnp.concatenate([seen[src, 1:3, :] for src in range(DEVS)], axis=0)
    in_lanes = jnp.sum(jnp.where(term == lane, full, 0.0), axis=0, keepdims=True)
    rank = jnp.sum(jnp.where(term < lane, full, 0.0), axis=0, keepdims=True)
    rank_down = jnp.sum(jnp.where(lane < term, in_lanes, 0.0), axis=1, keepdims=True)
    holder = jnp.sum(jnp.where(rank_down == lane.astype(f32), full * term.astype(f32), 0.0), axis=0, keepdims=True)
    table[...] = jnp.where(row == 1, holder, jnp.where(in_lanes > 0.5, rank, jnp.where(row == 0, FEW, TERMS).astype(f32))).astype(jnp.int32)
    few[0] = jnp.where(jnp.sum(in_lanes) < FEW + 0.5, 1, 0)
    pl.run_scoped(functools.partial(start_vector, norm), pltpu.VMEM((5, 128, 8, LANES), f32), pltpu.VMEM((8, 256, LANES), f32))
    slab_out = pltpu.make_async_copy(cur, slab_hbm, load_sem.at[1])
    slab_out.start()
    for off, dev in others():
        pair_copy(off, dev, dev).wait_recv()
    build_pairs()
    wi_out = pltpu.make_async_copy(wi, wi_hbm, load_sem.at[2])
    wi_out.start()
    net.take_pairs(left_view, net.at(0))
    net.take_last(left_view, net.at(0))
    net.chunk_ready(left_view, net.at(0))
    all_left = pltpu.make_async_copy(left, left_out, load_sem.at[3])
    all_left.start()
    net.drain_sends(left_view, net.at(0))
    for off, dev in others():
        right_copy(off, dev, dev).wait_recv()
    for off, dev in others():
        seen_copy(off, dev, me).wait_send()
        pair_copy(off, dev, me).wait_send()
        right_copy(off, dev, me).wait_send()
    right_own.wait()
    slab_out.wait()
    wi_out.wait()
    all_left.wait()
    for ch in range(CHUNKS):
        vector_out(ch).wait()


VECTOR_SHAPE = (CHUNKS, 8, 2, 2, 2, 2, 80, LANES)


def prepare(flags, psi, pair_loc, right_loc, left_loc):
    smem = pl.BlockSpec(memory_space=pltpu.SMEM)
    vmem = pl.BlockSpec(memory_space=pltpu.VMEM)
    hbm = pl.BlockSpec(memory_space=pltpu.HBM)
    dma = pltpu.SemaphoreType.DMA
    return pl.pallas_call(
        prep_kernel,
        out_shape=(
            jax.ShapeDtypeStruct((8, LANES), jnp.int32), jax.ShapeDtypeStruct((1,), jnp.int32), jax.ShapeDtypeStruct((1,), f32),
            jax.ShapeDtypeStruct(VECTOR_SHAPE, bf), jax.ShapeDtypeStruct((BOND, BOND), f32),
            jax.ShapeDtypeStruct((DEVS, 2, 256, 256), bf), jax.ShapeDtypeStruct((5, TERMS, SLAB, LANES), bf), jax.ShapeDtypeStruct((2, 2, 2, 2, 2, 128, BOND), bf),
        ),
        in_specs=[smem, hbm, hbm, vmem, hbm, hbm],
        out_specs=(vmem, smem, smem, hbm, hbm, hbm, hbm, hbm),
        scratch_shapes=[
            pltpu.VMEM(VECTOR_SHAPE, bf),
            pltpu.VMEM((5, 2 * BOND, LANES), bf),
            pltpu.VMEM((5, TERMS, SLAB, LANES), bf),
            pltpu.VMEM((BOND, BOND), f32),
            pltpu.VMEM((DEVS, 8, LANES), f32),
            pltpu.VMEM((DEVS, 2, PAIR, LANES), bf),
            pltpu.VMEM((DEVS, 2, 256, 256), bf),
            pltpu.VMEM((2, 2, 2, 2, 2, 128, BOND), bf),
            dma((8,)), dma((5,)), dma((CHUNKS,)), dma((DEVS,)), dma((DEVS,)), dma((2, DEVS)), dma((2, DEVS)),
            dma((1, 3, 7)), dma((1, 3, 7)), dma((1, 8)), dma((1, 8)),
        ],
        compiler_params=pltpu.CompilerParams(collective_id=0, has_side_effects=True, vmem_limit_bytes=67043328),
    )(flags, psi, psi.reshape(BOND * PAIR, BOND), pair_loc, right_loc.reshape(2 * BOND, BOND), left_loc)


def lanczos_kernel(most, table, u_hbm, slab_hbm, wi_hbm, right_hbm, first_left, left_hbm, gathered, alphas, betas,
                   u, lft, y, acc, cur, prev, ar, rc, wi,
                   load_sem, own_sem, ici_send, ici_recv, d2d_send, d2d_recv, ar_send, ar_recv, out_send, out_recv):
    me = lax.axis_index(AXIS_NAME)
    net = Gather(me, ici_send, ici_recv, d2d_send, d2d_recv)
    core, place = net.core, net.place

    def vec_view(ch, part, flips):
        pairs = PART_PAIRS[part] if part < 3 else (0, 8)
        return u.at[(ch, slice(pairs[0], pairs[1])) + net.slots(flips)]

    def left_view(ch, part, flips):
        lo, hi = LEFT_ROWS[part] if part < 3 else (0, 128)
        return lft.at[net.slots(flips) + (slice(None), slice(128 * ch + lo, 128 * ch + hi), slice(128 * ch, BOND))]

    def for_left(ch, what):
        for c in range(CHUNKS):
            @pl.when(ch == c)
            def _():
                what(left_view, net.at(c))

    def send_partial(which, partials):
        row = iota((8, LANES), 0)
        tile = jnp.zeros((8, LANES), f32)
        for n, partial in enumerate(partials):
            tile = jnp.where(row == n, jnp.sum(partial, axis=0, keepdims=True), tile)
        ar[which, me] = tile
        for off in range(1, DEVS):
            dev = lax.rem(me + off, DEVS)
            ref = ar.at[which, me]
            remote(ref, ref, ar_send.at[which, off], ar_recv.at[which, me], dev).start()

    def total_of(which, count):
        for off in range(1, DEVS):
            dev = lax.rem(me + off, DEVS)
            ref = ar.at[which, dev]
            remote(ref, ref, ar_send.at[which, off], ar_recv.at[which, dev], dev).wait_recv()
        total = jnp.sum(ar[which], axis=0)
        sums = [jnp.sum(total[n:n + 1]) / VEC_SIZE for n in range(count)]
        for off in range(1, DEVS):
            dev = lax.rem(me + off, DEVS)
            ref = ar.at[which, me]
            remote(ref, ref, ar_send.at[which, off], ar_recv.at[which, me], dev).wait_send()
        return sums

    def dots(fn, count):
        def body(g, tots):
            rows = pl.ds(pl.multiple_of(g * 16, 16), 16)
            out = []
            for tot, val in zip(tots, fn(rows)):
                for r in range(2):
                    for c in range(5):
                        tot = tot + val[8 * r:8 * r + 8, 128 * c:128 * c + 128]
                out.append(tot)
            return tuple(out)
        return lax.fori_loop(0, 40, body, (jnp.zeros((8, LANES), f32),) * count)

    def write_u():
        for ch in range(CHUNKS):
            lanes = slice(128 * ch, 128 * ch + 128)
            for i in range(8):
                dst = u.at[ch, i, place[2], place[1], place[0], core]
                dst[0:16] = cur[32 * i:32 * i + 16, lanes].astype(bf)
                dst[16:32] = cur[256 + 32 * i:256 + 32 * i + 16, lanes].astype(bf)
                dst[32:48] = cur[32 * i + 16:32 * i + 32, lanes].astype(bf)
                dst[48:64] = cur[256 + 32 * i + 16:256 + 32 * i + 32, lanes].astype(bf)
                dst[64:80] = cur[512 + 16 * i:512 + 16 * i + 16, lanes].astype(bf)

    def right_phase(ch, middle):
        for par in range(2):
            if par == 1:
                middle()
            rhs = []
            for i in range(8):
                main = u[ch, i, :, :, :, :, 32 * par:32 * par + 32, :].reshape(512, 128)
                tail = u[ch, i, :, :, :, :, 64:80, :].reshape(256, 128)
                rhs.append(jnp.concatenate([main, tail], axis=0))
            rhs = jnp.concatenate(rhs, axis=1)
            lhs = jnp.concatenate([rc[:, 0:512], rc[:, 512 + 256 * par:768 + 256 * par]], axis=1)
            val = jnp.dot(lhs, rhs, preferred_element_type=f32)
            for i in range(8):
                y[2 * i + par, 0:most] = val[:, 128 * i:128 * i + 128].reshape(most, SLAB, 128).astype(bf)
                own = u.at[ch, i, place[2], place[1], place[0], core]
                y[2 * i + par, most, 0:32] = own[32 * par:32 * par + 32, :]
                y[2 * i + par, most, 32:40] = own[64 + 8 * par:72 + 8 * par, :]

    def pair_left_phase(ch, zb, half_done):
        low_rows = (iota((256, 256), 0) & 15) < 8

        @pl.loop(0, 2)
        def _(g):
            for s in range(8):
                k = g * 8 + s
                first, second = [table[0 if most == FEW else 2, 2 * k + t] for t in range(2)]

                def tile(at, row):
                    return y[:, at, row:row + 16, :].reshape(256, 128)

                z01 = jnp.dot(wi[k, 0], jnp.concatenate([tile(first, 0), tile(first, 16)], axis=1), preferred_element_type=f32).astype(bf)
                mixed = jnp.where(low_rows, wi[k, 0], wi[k, 1])
                ends = jnp.concatenate([y[:, at, 32:40, :] for at in (first, second)], axis=1).reshape(256, 128)
                z2 = jnp.dot(mixed, ends, preferred_element_type=f32).reshape(16, 2, 8, 128)
                z34 = jnp.dot(wi[k, 1], jnp.concatenate([tile(second, 0), tile(second, 16)], axis=1), preferred_element_type=f32).astype(bf)
                zb[s, 0:256, 0:128] = z01[:, 0:128]
                zb[s, 256:512, 0:128] = z01[:, 128:256]
                zb[s, 512:640, 0:128] = z2[:, 0].reshape(128, 128).astype(bf)
                zb[s, 0:256, 128:256] = z34[:, 0:128]
                zb[s, 256:512, 128:256] = z34[:, 128:256]
                zb[s, 512:640, 128:256] = z2[:, 1].reshape(128, 128).astype(bf)
            lhs = jnp.concatenate([zb[s] for s in range(8)], axis=1)
            rows = pl.ds(pl.multiple_of(ch * 128, 128), 128)
            rhs = jnp.concatenate([lft[g, s // 4, s // 2 % 2, s % 2, t, rows, :] for s in range(8) for t in range(2)], axis=0)
            acc[...] += jnp.dot(lhs, rhs, preferred_element_type=f32)

            @pl.when(g == 0)
            def _():
                half_done()

    def turn(vec, turned):
        shifted = [lax.rem(q + DEVS - me, DEVS) for q in range(PAIR)]
        for lt in range(5):
            rows = []
            for n in range(16 * lt, 16 * lt + 16):
                q, part = shifted[n // 5], n % 5
                start = 512 + 8 * q if part == 4 else 256 * (part // 2) + 16 * q + 8 * (part % 2)
                rows.append(vec[pl.ds(pl.multiple_of(start, 8), 8), :])
            turned[:, 128 * lt:128 * lt + 128] = jnp.concatenate(rows, axis=0).T

    def flipped(mask):
        dev = me
        for n, bit in enumerate((core,) + place):
            if mask >> n & 1:
                dev = dev + (1 << n) * (1 - 2 * bit)
        return dev

    def out_copy(turned, vec, mask, final, arriving=False):
        dev = flipped(mask)
        src = dev if arriving else me
        rows = pl.ds(pl.multiple_of(dev * SLAB, 8), SLAB)
        return remote(turned.at[rows], gathered.at[vec, src], out_send.at[mask], out_recv.at[final, mask], dev)

    def own_copy(turned, vec):
        rows = pl.ds(pl.multiple_of(me * SLAB, 8), SLAB)
        return pltpu.make_async_copy(turned.at[rows], gathered.at[vec, me], own_sem)

    def send_out(turned, vec, masks, final=0):
        for mask in masks:
            out_copy(turned, vec, mask, final).start()

    def finish_out(turned, vec, final=0):
        own_copy(turned, vec).wait()
        for mask in range(1, DEVS):
            out_copy(turned, vec, mask, final, True).wait_recv()
        for mask in range(1, DEVS):
            out_copy(turned, vec, mask, final).wait_send()

    def build_right():
        for n in range(most):
            for t in range(5):
                rc[SLAB * n:SLAB * n + SLAB, 128 * t:128 * t + 128] = y[t, table[1, n]]
        tails = rc[:, 512:640]
        src = iota((128, 256), 0)
        spot = 16 * (src >> 3) + (src & 7)
        for par in range(2):
            widen = (spot + 8 * par == iota((128, 256), 1)).astype(bf)
            rc[:, 512 + 256 * par:768 + 256 * par] = jnp.dot(tails, widen, preferred_element_type=f32).astype(bf)

    def mirror_left(ch):
        @pl.loop(0, 8)
        def _(g):
            for n in range(4):
                at = (g // 4, lax.rem(g // 2, 2), lax.rem(g, 2), n // 2, n % 2)
                for other in range(ch + 1, CHUNKS):
                    block = lft[at + (slice(128 * ch, 128 * ch + 128), slice(128 * other, 128 * other + 128))]
                    lft[at + (slice(128 * other, 128 * other + 128), slice(128 * ch, 128 * ch + 128))] = block.T

    left_load = pltpu.make_async_copy(left_hbm.at[:, 128:BOND], lft.at[net.slots(()) + (slice(None), slice(128, BOND))], load_sem.at[0])
    right_load = pltpu.make_async_copy(right_hbm, y.at[0:5, 0:TERMS], load_sem.at[1])
    wi_load = pltpu.make_async_copy(wi_hbm, wi, load_sem.at[2])
    slab_load = pltpu.make_async_copy(slab_hbm, cur, load_sem.at[3])
    first_load = pltpu.make_async_copy(first_left, lft.at[:, :, :, :, :, 0:128], load_sem.at[4])

    def vector_load(ch):
        return pltpu.make_async_copy(u_hbm.at[ch], u.at[ch], load_sem.at[5 + ch])

    left_load.start()
    right_load.start()
    vector_load(0).start()
    wi_load.start()
    first_load.start()
    for ch in range(1, CHUNKS):
        vector_load(ch).start()
    slab_load.start()
    entry_barrier(me)
    left_load.wait()
    net.own_out(left_view, net.at(1))
    right_load.wait()
    build_right()
    prev[...] = jnp.zeros_like(prev)

    def step(zb, turned, j, beta_prev):
        acc[...] = jnp.zeros_like(acc)

        later = j > 0

        @pl.when(later)
        def _():
            zero, one = net.at(0), net.at(1)
            net.own_out(vec_view, zero)
            turn(cur, turned)
            own_copy(turned, j - 1).start()
            net.relay_first(vec_view, zero)
            net.relay_second(vec_view, zero)
            net.relay_last(vec_view, zero)
            net.own_out(vec_view, one)
            net.relay_third(vec_view, zero)
            net.take_pairs(vec_view, zero)
            net.take_last(vec_view, zero)
            net.chunk_ready(vec_view, zero)

        @pl.loop(0, CHUNKS)
        def _(ch):
            next_spot, after_spot = net.at(ch + 1), net.at(ch + 2)

            @pl.when(later & (ch + 1 < CHUNKS))
            def _():
                net.relay_first(vec_view, next_spot)

            @pl.when(later & (ch == 4))
            def _():
                send_out(turned, j - 1, (7, 13, 11))

            def middle():
                @pl.when(later & (ch + 1 < CHUNKS))
                def _():
                    net.relay_second(vec_view, next_spot)

            @pl.when(j == 0)
            def _():
                vector_load(ch).wait()

            right_phase(ch, middle)

            @pl.when(later & (ch + 1 < CHUNKS))
            def _():
                net.relay_third(vec_view, next_spot)
                net.relay_last(vec_view, next_spot)

                @pl.when(ch + 2 < CHUNKS)
                def _():
                    net.own_out(vec_view, after_spot)

                @pl.when(ch == 3)
                def _():
                    send_out(turned, j - 1, (1, 3, 5, 9, 14, 15))

            @pl.when(j == 0)
            def _():
                @pl.when(ch == 0)
                def _():
                    wi_load.wait()
                    first_load.wait()

                def left_ready(view, spot):
                    if spot.ch > 0:
                        mirror_left(spot.ch - 1)
                        net.take_pairs(view, spot)
                        net.take_last(view, spot)
                        net.chunk_ready(view, spot)

                for_left(ch, left_ready)
                for_left(ch + 1, net.relay_first)

            def half_done():
                @pl.when(later & (ch + 1 < CHUNKS))
                def _():
                    net.take_pairs(vec_view, next_spot)
                    net.take_last(vec_view, next_spot)

                    @pl.when(ch == 2)
                    def _():
                        send_out(turned, j - 1, (2, 4, 8))

                    @pl.when(ch == 3)
                    def _():
                        send_out(turned, j - 1, (6, 12, 10))

                @pl.when(j == 0)
                def _():
                    for_left(ch + 1, net.relay_second)

            pair_left_phase(ch, zb, half_done)

            @pl.when(later & (ch + 1 < CHUNKS))
            def _():
                net.chunk_ready(vec_view, next_spot)

            @pl.when(j == 0)
            def _():
                def advance(view, spot):
                    net.relay_third(view, spot)
                    net.relay_last(view, spot)

                for_left(ch + 1, advance)
                for_left(ch + 2, net.own_out)

        @pl.loop(0, CHUNKS)
        def _(ch):
            @pl.when((j == 0) & (ch > 0))
            def _():
                for_left(ch, net.drain_sends)

            @pl.when(later)
            def _():
                net.drain_sends(vec_view, net.at(ch))

        @pl.when(later)
        def _():
            finish_out(turned, j - 1)

        @pl.when(j == 0)
        def _():
            slab_load.wait()

        @pl.when(j == 0)
        def _():
            send_partial(0, dots(lambda rows: (acc[rows, :] * cur[rows, :],), 1))
            betas[0, LANCZOS_STEPS + 1] = total_of(0, 1)[0]

        shift = betas[0, LANCZOS_STEPS + 1]

        def products(rows):
            v, v_prev = cur[rows, :], prev[rows, :]
            w = acc[rows, :] - shift * v - beta_prev * v_prev
            acc[rows, :] = w
            return w * w, w * v, v * v, v * v_prev

        send_partial(1, dots(products, 4))

        @pl.when(j + 1 == LANCZOS_STEPS)
        def _():
            turn(acc, turned)
            own_copy(turned, j).start()
            send_out(turned, j, (14, 15, 6, 12, 10, 7, 13, 11, 2, 4, 8, 3, 5, 9, 1), 1)

        ww, wv, vv, vp = total_of(1, 4)
        alpha = wv + shift * vv + beta_prev * vp
        extra = alpha - shift
        beta = jnp.sqrt(ww - 2.0 * extra * wv + extra * extra * vv)
        alphas[0, j] = alpha
        betas[0, j] = beta
        betas[0, LANCZOS_STEPS] = extra
        betas[0, LANCZOS_STEPS + 1] = alpha

        @pl.when(j + 1 < LANCZOS_STEPS)
        def _():
            @pl.loop(0, 40)
            def _(g):
                rows = pl.ds(pl.multiple_of(g * 16, 16), 16)
                v = cur[rows, :]
                prev[rows, :] = v
                cur[rows, :] = (acc[rows, :] - extra * v) / beta

            write_u()

        return beta

    def all_steps(zb, turned):
        lax.fori_loop(0, LANCZOS_STEPS, functools.partial(step, zb, turned), jnp.zeros((), f32))
        finish_out(turned, LANCZOS_STEPS - 1, 1)

    pl.run_scoped(all_steps, pltpu.VMEM((8, BOND, 256), bf), pltpu.VMEM((BOND, BOND), f32))


def run_lanczos(most, table, u_hbm, slab_hbm, wi_hbm, right_hbm, first_left, left_loc):
    smem = pl.BlockSpec(memory_space=pltpu.SMEM)
    hbm = pl.BlockSpec(memory_space=pltpu.HBM)
    dma = pltpu.SemaphoreType.DMA
    return pl.pallas_call(
        functools.partial(lanczos_kernel, most),
        out_shape=(jax.ShapeDtypeStruct((LANCZOS_STEPS, DEVS, SLAB, BOND), f32), jax.ShapeDtypeStruct((1, 8), f32), jax.ShapeDtypeStruct((1, 8), f32)),
        in_specs=[smem] + [hbm] * 6,
        out_specs=(hbm, smem, smem),
        scratch_shapes=[
            pltpu.VMEM(VECTOR_SHAPE, bf),
            pltpu.VMEM((2, 2, 2, 2, 2, BOND, BOND), bf),
            pltpu.VMEM((PAIR, TERMS + 1, SLAB, LANES), bf),
            pltpu.VMEM((BOND, BOND), f32),
            pltpu.VMEM((BOND, BOND), f32),
            pltpu.VMEM((BOND, BOND), f32),
            pltpu.VMEM((2, DEVS, 8, LANES), f32),
            pltpu.VMEM((most * SLAB, 1024), bf),
            pltpu.VMEM((DEVS, 2, 256, 256), bf),
            dma((5 + CHUNKS,)), dma, dma((CHUNKS, 3, 7)), dma((CHUNKS, 3, 7)), dma((CHUNKS, 8)), dma((CHUNKS, 8)),
            dma((2, DEVS)), dma((2, DEVS)), dma((DEVS,)), dma((2, DEVS)),
        ],
        compiler_params=pltpu.CompilerParams(collective_id=most, has_side_effects=True, vmem_limit_bytes=67043328),
    )(table, u_hbm, slab_hbm, wi_hbm, right_hbm, first_left, left_loc)


def place_kernel(norm, alphas, betas, psi, gathered, krylov, alpha_out, beta_out, rows, src, dst, load_sem, store_sem):
    me = lax.axis_index(AXIS_NAME)

    def load(vec):
        return pltpu.make_async_copy(gathered.at[vec], src.at[vec], load_sem.at[vec])

    def store(vec):
        return pltpu.make_async_copy(dst.at[vec], krylov.at[vec], store_sem.at[vec])

    def placed(vec, r, q):
        lane = iota((8, LANES), 1)
        tiles = []
        for t in range(5):
            tile = None
            for m in range(128 * t // SLAB, min(DEVS, (128 * t + 127) // SLAB + 1)):
                val = src[vec, (m - q) % DEVS, pl.ds(r, 8), 128 * t:128 * t + 128]
                tile = val if tile is None else jnp.where(lane >= SLAB * m - 128 * t, val, tile)
            tiles.append(tile)
        skip, rest = SLAB * q // 128, SLAB * q % 128
        if rest:
            tiles = [pltpu.roll(tile, 128 - rest, 1) for tile in tiles]
        tiles = [tiles[(t + skip) % 5] if not rest else jnp.where(lane < 128 - rest, tiles[(t + skip) % 5], tiles[(t + skip + 1) % 5]) for t in range(5)]
        return jnp.concatenate(tiles, axis=1)

    rows_load = pltpu.make_async_copy(psi.at[pl.ds(me * SLAB, SLAB)], rows, load_sem.at[LANCZOS_STEPS])
    rows_load.start()
    for vec in range(LANCZOS_STEPS):
        load(vec).start()
    for n in range(LANCZOS_STEPS):
        alpha_out[n] = alphas[0, n]
        beta_out[n] = betas[0, n]
    rows_load.wait()
    dst[0] = rows[...] / norm[0]
    store(0).start()

    @pl.loop(0, LANCZOS_STEPS - 1)
    def _(vec):
        load(vec).wait()
        for r in range(0, SLAB, 8):
            for q in range(PAIR):
                dst[vec + 1, r:r + 8, q, :] = placed(vec, r, q)
        store(vec + 1).start()

    load(LANCZOS_STEPS - 1).wait()
    for r in range(0, SLAB, 8):
        for q in range(PAIR):
            before = dst[LANCZOS_STEPS - 1, r:r + 8, q, :]
            dst[LANCZOS_STEPS, r:r + 8, q, :] = (placed(LANCZOS_STEPS - 1, r, q) - betas[0, LANCZOS_STEPS] * before) / betas[0, LANCZOS_STEPS - 1]
    store(LANCZOS_STEPS).start()
    for vec in range(LANCZOS_STEPS + 1):
        store(vec).wait()


def place_outputs(norm, alphas, betas, wavefunction, gathered):
    smem = pl.BlockSpec(memory_space=pltpu.SMEM)
    hbm = pl.BlockSpec(memory_space=pltpu.HBM)
    dma = pltpu.SemaphoreType.DMA
    return pl.pallas_call(
        place_kernel,
        out_shape=(jax.ShapeDtypeStruct((LANCZOS_STEPS + 1, SLAB, PAIR, BOND), f32), jax.ShapeDtypeStruct((LANCZOS_STEPS,), f32), jax.ShapeDtypeStruct((LANCZOS_STEPS,), f32)),
        in_specs=[smem, smem, smem, hbm, hbm],
        out_specs=(hbm, smem, smem),
        scratch_shapes=[
            pltpu.VMEM((SLAB, PAIR, BOND), f32),
            pltpu.VMEM((LANCZOS_STEPS, DEVS, SLAB, BOND), f32),
            pltpu.VMEM((LANCZOS_STEPS + 1, SLAB, PAIR, BOND), f32),
            dma((LANCZOS_STEPS + 1,)), dma((LANCZOS_STEPS + 1,)),
        ],
        compiler_params=pltpu.CompilerParams(vmem_limit_bytes=40 * 1024 * 1024),
    )(norm, alphas, betas, wavefunction, gathered)


def solution(mesh):
    def device_body(wavefunction, left_loc, pair_loc, right_loc, flag_loc):
        table, few, norm, *operands = prepare(flag_loc, wavefunction, pair_loc, right_loc, left_loc)
        few_full, all_full = functools.partial(run_lanczos, FEW), functools.partial(run_lanczos, TERMS)
        vecs, alphas, betas = lax.cond(few[0] == 1, few_full, all_full, table, *operands, left_loc)
        return place_outputs(norm, alphas, betas, wavefunction, vecs)

    return jax.shard_map(device_body, mesh=mesh, in_specs=(P(), P(AXIS_NAME), P(AXIS_NAME), P(AXIS_NAME), P(AXIS_NAME)), out_specs=(P(None, AXIS_NAME), P(), P()), check_vma=False)
```

time: 3730 us -> 524 us (0.14)
  waiting for transfers between devices: 2170 us -> 0 us
  local copies, waits for them, and re-layouts: 560 us -> 0 us
  Pallas kernels: 0 us -> 522 us
  matrix products: 483 us -> 0 us
  blocking collectives: 382 us -> 0 us
  other arithmetic: 88.7 us -> 0 us
    reduce_scatter x6 -> x0, waiting for transfers between devices: 1850 us -> none  [device_body(): lax.psum_scatter(part_sigma, AXIS_NAME, scatter_dimension=0, tiled=True)]
    pallas_call x0 -> x3, Pallas kernels: none -> 522 us  [the longest x1 459 us: run_lanczos(): pl.pallas_call(functools.partial(lanczos_kernel, most), out_shape=(jax.Sh...]
    dot_general x24 -> x0, matrix products: 483 us -> none  [the longest x12 327 us: term_body(): lax.dot_general(left_loc[term_idx], pair_done, (((1,), (1,)), ((), ())),...]
    psum x12 -> x0, blocking collectives: 382 us -> none  [the longest x6 196 us: device_body(): lax.psum(jnp.sum(residual * residual), AXIS_NAME) / vec_size]
    all_gather x5 -> x0, waiting for transfers between devices: 325 us -> none  [device_body(): lax.all_gather(following.astype(jnp.bfloat16), AXIS_NAME, axis=0, tiled=T...]
    cond x12 -> x0, local copies, waits for them, and re-layouts: 279 us -> none  [term_body(): lax.cond(flag_loc[term_idx] == 1, apply_right, keep_vector, right_loc[ter...]
    while x6 -> x0, local copies, waits for them, and re-layouts: 197 us -> none  [local_sigma(): return lax.fori_loop(0, left_loc.shape[0], term_body, start_sum)]
    unnamed x44 -> x0, local copies, waits for them, and re-layouts: 75.6 us -> none
  transfers between devices with their start and end apart: 11 -> 0, of which waited for: 11 -> 0; matrix products, arithmetic and copies ran while one was open for 0% -> 0% of each run, Pallas kernels for 0% -> 0%
where the time goes in v3:
time: 524 us
  Pallas kernels  522 us (100%)
    pallas_call x1, Pallas kernels, run_lanczos(): pl.pallas_call(functools.partial(lanczos_kernel, most), out_shape=(jax.Sh...  459 us
    pallas_call x1, Pallas kernels, prepare(): pl.pallas_call(prep_kernel, out_shape=(jax.ShapeDtypeStruct((8, LANES), j...  50.6 us
    pallas_call x1, Pallas kernels, place_outputs(): pl.pallas_call(place_kernel, out_shape=(jax.ShapeDtypeStruct((LANCZOS_STE...  11.9 us

profile of v3, /device:TPU:0, one launch (start us, length us, event | category | flops | bytes accessed | tf_op | source)
XLA Modules:
  0.0 523.5 jit_solution(10892046717261625450)
XLA Ops:
  0.6 50.6 %shard_map.76 = (s32[8,128]{1,0:T(8,128)}, s32[1]{0:T(128)}, f32[1]{0:T(128)}, bf16[5,8,2,2,2,2,80,128]{7,6,5,4,3,2,1,0:T(8,128)(2,1)}, f32[640,640]{1,0:T(8,128...) custom-call(s32[2]{0:T(128)} %flags.1, ...), custom_call_target="tpu_custom_call" | custom-call | tf_op jit(solution)/shard_map/pallas_call | solution.py:351
  51.9 459.6 %conditional.1 = ((f32[6,16,40,640]{3,2,1,0:T(8,128)}, f32[1,8]{1,0:T(1,128)}, f32[1,8]{1,0:T(1,128)})) conditional(s32[]{:T(128)} %bitcast.2, (s32[8,128]{1,0:T(8,128)}, bf16[5,8,2,2,2,2,80,128]{7,6,5,4,3,2,1,0:T(8,128)(2,1)}, f32[640,640]{1,0:T(8,128)}, bf16[16,2,256,256]{3,2,1,0:T(8,128)(2,1)}, bf16[5,32,40,128]{3,2,1,0:T(8,128)(2,1)}, ...), branch_computations={%region_0.0_spmd, %region_1.0_spmd} | conditional | bytes 8 | solution.py:852
  52.3 459.1 %branch_1_fun.1 = (f32[6,16,40,640]{3,2,1,0:T(8,128)}, f32[1,8]{1,0:T(1,128)}, f32[1,8]{1,0:T(1,128)}) custom-call(s32[8,128]{1,0:T(8,128)} %get-tuple-element.35.table, bf16[5,8,2,2,2,2,80,128]{7,6,5,4,3,2,1,0:T(8,128)(2,1)} %get-tuple-element.36.u_hbm, f32[640,640]{1,0:T(8,128)} %get-tuple-element.37.slab_hbm, ...), custom_call_target="tpu_custom_call" | custom-call | tf_op jit(solution)/shard_map/cond/branch_1_fun/pallas_call | solution.py:754
  511.5 11.9 %shard_map.77 = (f32[7,40,16,640]{3,2,1,0:T(8,128)}, f32[6]{0:T(128)}, f32[6]{0:T(128)}) custom-call(f32[1]{0:T(128)} %get-tuple-element.56.norm, f32[1,8]{1,0:T(1,128)} %get-tuple-element.64.alphas, f32[1,8]{1,0:T(1,128)} %get-tuple-element.65.betas, f32[640,16,640]{2,1,0:T(8,128)} %psi.3, f32[6,16,40,640]{3,2,1,0:T(8,128)} %get-tuple-element.66.gathered), custom_call_target="tpu_custom_call" | custom-call | tf_op jit(solution)/shard_map/pallas_call | solution.py:833

commit v4 on v3

--- a/solution.py
+++ b/solution.py
@@ -574,8 +574,6 @@
     prev[...] = jnp.zeros_like(prev)
 
     def step(zb, turned, j, beta_prev):
-        acc[...] = jnp.zeros_like(acc)
-
         later = j > 0
 
         @pl.when(later)
@@ -591,7 +589,10 @@
             net.relay_third(vec_view, zero)
             net.take_pairs(vec_view, zero)
             net.take_last(vec_view, zero)
+            net.relay_first(vec_view, one)
             net.chunk_ready(vec_view, zero)
+
+        acc[...] = jnp.zeros_like(acc)
 
         @pl.loop(0, CHUNKS)
         def _(ch):
@@ -599,35 +600,39 @@
 
             @pl.when(later & (ch + 1 < CHUNKS))
             def _():
-                net.relay_first(vec_view, next_spot)
+                net.relay_second(vec_view, next_spot)
 
             @pl.when(later & (ch == 4))
             def _():
                 send_out(turned, j - 1, (7, 13, 11))
+
+            @pl.when(j == 0)
+            def _():
+                vector_load(ch).wait()
 
             def middle():
                 @pl.when(later & (ch + 1 < CHUNKS))
                 def _():
-                    net.relay_second(vec_view, next_spot)
-
-            @pl.when(j == 0)
-            def _():
-                vector_load(ch).wait()
+                    net.relay_third(vec_view, next_spot)
+                    net.relay_last(vec_view, next_spot)
+
+                    @pl.when(ch + 2 < CHUNKS)
+                    def _():
+                        net.own_out(vec_view, after_spot)
+
+                    @pl.when(ch == 3)
+                    def _():
+                        send_out(turned, j - 1, (1, 3, 5, 9, 14, 15))
+
+                @pl.when((j == 0) & (ch > 0))
+                def _():
+                    def take(view, spot):
+                        net.take_pairs(view, spot)
+                        net.take_last(view, spot)
+
+                    for_left(ch, take)
 
             right_phase(ch, middle)
-
-            @pl.when(later & (ch + 1 < CHUNKS))
-            def _():
-                net.relay_third(vec_view, next_spot)
-                net.relay_last(vec_view, next_spot)
-
-                @pl.when(ch + 2 < CHUNKS)
-                def _():
-                    net.own_out(vec_view, after_spot)
-
-                @pl.when(ch == 3)
-                def _():
-                    send_out(turned, j - 1, (1, 3, 5, 9, 14, 15))
 
             @pl.when(j == 0)
             def _():
@@ -639,8 +644,6 @@
                 def left_ready(view, spot):
                     if spot.ch > 0:
                         mirror_left(spot.ch - 1)
-                        net.take_pairs(view, spot)
-                        net.take_last(view, spot)
                         net.chunk_ready(view, spot)
 
                 for_left(ch, left_ready)
@@ -652,6 +655,10 @@
                     net.take_pairs(vec_view, next_spot)
                     net.take_last(vec_view, next_spot)
 
+                    @pl.when(ch + 2 < CHUNKS)
+                    def _():
+                        net.relay_first(vec_view, after_spot)
+
                     @pl.when(ch == 2)
                     def _():
                         send_out(turned, j - 1, (2, 4, 8))
@@ -688,10 +695,6 @@
             @pl.when(later)
             def _():
                 net.drain_sends(vec_view, net.at(ch))
-
-        @pl.when(later)
-        def _():
-            finish_out(turned, j - 1)
 
         @pl.when(j == 0)
         def _():
@@ -711,6 +714,10 @@
             return w * w, w * v, v * v, v * v_prev
 
         send_partial(1, dots(products, 4))
+
+        @pl.when(later)
+        def _():
+            finish_out(turned, j - 1)
 
         @pl.when(j + 1 == LANCZOS_STEPS)
         def _():

time: 524 us -> 505 us (0.964)
  Pallas kernels: 522 us -> 502 us
    pallas_call x1, Pallas kernels: 459 us -> 440 us  [run_lanczos(): pl.pallas_call(functools.partial(lanczos_kernel, most), out_shape=(jax.Sh...]
where the time goes in v4:
time: 505 us; the launch traced here: 504 us
  Pallas kernels  502 us (99%)
    pallas_call x1, Pallas kernels, run_lanczos(): pl.pallas_call(functools.partial(lanczos_kernel, most), out_shape=(jax.Sh...  440 us
    pallas_call x1, Pallas kernels, prepare(): pl.pallas_call(prep_kernel, out_shape=(jax.ShapeDtypeStruct((8, LANES), j...  50.6 us
    pallas_call x1, Pallas kernels, place_outputs(): pl.pallas_call(place_kernel, out_shape=(jax.ShapeDtypeStruct((LANCZOS_STE...  11.9 us

profile of v4, /device:TPU:0, one launch (start us, length us, event | category | flops | bytes accessed | tf_op | source)
XLA Modules:
  0.0 504.3 jit_solution(14333413107681978319)
XLA Ops:
  0.6 50.6 %shard_map.76 = (s32[8,128]{1,0:T(8,128)}, s32[1]{0:T(128)}, f32[1]{0:T(128)}, bf16[5,8,2,2,2,2,80,128]{7,6,5,4,3,2,1,0:T(8,128)(2,1)}, f32[640,640]{1,0:T(8,128...) custom-call(s32[2]{0:T(128)} %flags.1, ...), custom_call_target="tpu_custom_call" | custom-call | tf_op jit(solution)/shard_map/pallas_call | solution.py:351
  51.9 440.4 %conditional.1 = ((f32[6,16,40,640]{3,2,1,0:T(8,128)}, f32[1,8]{1,0:T(1,128)}, f32[1,8]{1,0:T(1,128)})) conditional(s32[]{:T(128)} %bitcast.2, (s32[8,128]{1,0:T(8,128)}, bf16[5,8,2,2,2,2,80,128]{7,6,5,4,3,2,1,0:T(8,128)(2,1)}, f32[640,640]{1,0:T(8,128)}, bf16[16,2,256,256]{3,2,1,0:T(8,128)(2,1)}, bf16[5,32,40,128]{3,2,1,0:T(8,128)(2,1)}, ...), branch_computations={%region_0.0_spmd, %region_1.0_spmd} | conditional | bytes 8 | solution.py:859
  52.3 440.0 %branch_1_fun.1 = (f32[6,16,40,640]{3,2,1,0:T(8,128)}, f32[1,8]{1,0:T(1,128)}, f32[1,8]{1,0:T(1,128)}) custom-call(s32[8,128]{1,0:T(8,128)} %get-tuple-element.35.table, bf16[5,8,2,2,2,2,80,128]{7,6,5,4,3,2,1,0:T(8,128)(2,1)} %get-tuple-element.36.u_hbm, f32[640,640]{1,0:T(8,128)} %get-tuple-element.37.slab_hbm, ...), custom_call_target="tpu_custom_call" | custom-call | tf_op jit(solution)/shard_map/cond/branch_1_fun/pallas_call | solution.py:761
  492.3 11.9 %shard_map.77 = (f32[7,40,16,640]{3,2,1,0:T(8,128)}, f32[6]{0:T(128)}, f32[6]{0:T(128)}) custom-call(f32[1]{0:T(128)} %get-tuple-element.56.norm, f32[1,8]{1,0:T(1,128)} %get-tuple-element.64.alphas, f32[1,8]{1,0:T(1,128)} %get-tuple-element.65.betas, f32[640,16,640]{2,1,0:T(8,128)} %psi.3, f32[6,16,40,640]{3,2,1,0:T(8,128)} %get-tuple-element.66.gathered), custom_call_target="tpu_custom_call" | custom-call | tf_op jit(solution)/shard_map/pallas_call | solution.py:840

commit v5 on v4

--- a/solution.py
+++ b/solution.py
@@ -14,7 +14,8 @@
 DEVS = 16
 SLAB = BOND // DEVS
 CHUNKS = 5
-FEW = 20
+FEWER, FEW = 16, 20
+TABLE_ROW = {16: 0, 20: 2, 32: 3}
 LANES = 128
 VEC_SIZE = BOND * PAIR * BOND
 bf = jnp.bfloat16
@@ -130,9 +131,12 @@
         self.wait_units(view, spot, 6)
         self.d2d(view, spot, 6).start()
 
+    def wait_d2d(self, view, spot, *which):
+        for n in which:
+            self.d2d(view, spot, n).wait_recv()
+
     def chunk_ready(self, view, spot):
-        for n in range(8):
-            self.d2d(view, spot, n).wait_recv()
+        self.wait_d2d(view, spot, *range(8))
 
     def drain_sends(self, view, spot):
         for n in range(8):
@@ -143,7 +147,7 @@
 
 
 def prep_kernel(flags, psi, psi_rows, pair_loc, right_hbm, left_hbm, table, few, norm_out, u_hbm, slab_hbm, wi_hbm, right_out, left_out,
-                u, y, moved, cur, seen, ops, wi, left, load_sem, stage_sem, out_sem, seen_send, seen_recv, op_send, op_recv, ici_send, ici_recv, d2d_send, d2d_recv):
+                u, y, moved, cur, seen, ops, wi, left, load_sem, stage_sem, out_sem, seen_send, seen_recv, op_send, op_recv, ici_send, ici_recv, d2d_send, d2d_recv, left_sem, small_i, small_f):
     me = lax.axis_index(AXIS_NAME)
     net = Gather(me, ici_send, ici_recv, d2d_send, d2d_recv)
 
@@ -153,15 +157,17 @@
 
     def dots(fn, count):
         def body(g, tots):
-            rows = pl.ds(pl.multiple_of(g * 16, 16), 16)
+            vals = fn(pl.ds(pl.multiple_of(g * 32, 32), 32))
             out = []
-            for tot, val in zip(tots, fn(rows)):
-                for r in range(2):
+            for n, val in enumerate(vals):
+                two = [tots[2 * n], tots[2 * n + 1]]
+                for r in range(4):
                     for c in range(5):
-                        tot = tot + val[8 * r:8 * r + 8, 128 * c:128 * c + 128]
-                out.append(tot)
+                        two[r % 2] = two[r % 2] + val[8 * r:8 * r + 8, 128 * c:128 * c + 128]
+                out += two
             return tuple(out)
-        return lax.fori_loop(0, 40, body, (jnp.zeros((8, LANES), f32),) * count)
+        tots = lax.fori_loop(0, 20, body, (jnp.zeros((8, LANES), f32),) * (2 * count))
+        return [tots[2 * n] + tots[2 * n + 1] for n in range(count)]
 
     def spread_right():
         col = iota((BOND, 128), 0)
@@ -218,6 +224,8 @@
             @pl.when(it == 6)
             def _():
                 net.relay_third(left_view, net.at(0))
+                for n in (7, 0, 1, 2):
+                    left_store(n).start()
 
             @pl.when(it == 8)
             def _():
@@ -254,6 +262,11 @@
             @pl.when(half == 1)
             def _():
                 vector_out(ch).start()
+
+    def left_store(n, other=False):
+        at = net.slots([AXES[m] for m in D2D_FLIPS[n]])
+        at = at[:3] + ((1 - net.core,) if other else at[3:])
+        return pltpu.make_async_copy(left.at[at], left_out.at[at], left_sem.at[int(other), n])
 
     def seen_copy(off, dev, src):
         return remote(seen.at[src], seen.at[src], seen_send.at[off], seen_recv.at[src], dev)
@@ -303,15 +316,20 @@
     for off, dev in others():
         seen_copy(off, dev, dev).wait_recv()
     norm = jnp.sqrt(jnp.sum(jnp.sum(seen[:, 0:1, :], axis=0)) / VEC_SIZE)
-    norm_out[0] = norm
+    small_f[...] = jnp.zeros((8, LANES), f32) + norm
+    norm_store = pltpu.make_async_copy(small_f, norm_out, load_sem.at[6])
+    norm_store.start()
     term, lane = iota((TERMS, LANES), 0), iota((TERMS, LANES), 1)
     full = jnp.concatenate([seen[src, 1:3, :] for src in range(DEVS)], axis=0)
     in_lanes = jnp.sum(jnp.where(term == lane, full, 0.0), axis=0, keepdims=True)
     rank = jnp.sum(jnp.where(term < lane, full, 0.0), axis=0, keepdims=True)
     rank_down = jnp.sum(jnp.where(lane < term, in_lanes, 0.0), axis=1, keepdims=True)
     holder = jnp.sum(jnp.where(rank_down == lane.astype(f32), full * term.astype(f32), 0.0), axis=0, keepdims=True)
-    table[...] = jnp.where(row == 1, holder, jnp.where(in_lanes > 0.5, rank, jnp.where(row == 0, FEW, TERMS).astype(f32))).astype(jnp.int32)
-    few[0] = jnp.where(jnp.sum(in_lanes) < FEW + 0.5, 1, 0)
+    small_i[...] = jnp.where(row == 1, holder, jnp.where(in_lanes > 0.5, rank, jnp.where(row == 0, FEWER, jnp.where(row == 2, FEW, TERMS)).astype(f32))).astype(jnp.int32)
+    count = jnp.sum(in_lanes)
+    few[0] = jnp.where(count < FEW + 0.5, 0, 1)
+    table_store = pltpu.make_async_copy(small_i, table, load_sem.at[7])
+    table_store.start()
     pl.run_scoped(functools.partial(start_vector, norm), pltpu.VMEM((5, 128, 8, LANES), f32), pltpu.VMEM((8, 256, LANES), f32))
     slab_out = pltpu.make_async_copy(cur, slab_hbm, load_sem.at[1])
     slab_out.start()
@@ -321,10 +339,16 @@
     wi_out = pltpu.make_async_copy(wi, wi_hbm, load_sem.at[2])
     wi_out.start()
     net.take_pairs(left_view, net.at(0))
+    for n in (3, 4, 5):
+        left_store(n).start()
+    net.wait_d2d(left_view, net.at(0), 7, 0, 1, 2)
+    for n in (7, 0, 1, 2):
+        left_store(n, True).start()
     net.take_last(left_view, net.at(0))
-    net.chunk_ready(left_view, net.at(0))
-    all_left = pltpu.make_async_copy(left, left_out, load_sem.at[3])
-    all_left.start()
+    left_store(6).start()
+    net.wait_d2d(left_view, net.at(0), 3, 4, 5, 6)
+    for n in (3, 4, 5, 6):
+        left_store(n, True).start()
     net.drain_sends(left_view, net.at(0))
     for off, dev in others():
         right_copy(off, dev, dev).wait_recv()
@@ -335,7 +359,11 @@
     right_own.wait()
     slab_out.wait()
     wi_out.wait()
-    all_left.wait()
+    norm_store.wait()
+    table_store.wait()
+    for n in range(8):
+        left_store(n).wait()
+        left_store(n, True).wait()
     for ch in range(CHUNKS):
         vector_out(ch).wait()
 
@@ -351,12 +379,12 @@
     return pl.pallas_call(
         prep_kernel,
         out_shape=(
-            jax.ShapeDtypeStruct((8, LANES), jnp.int32), jax.ShapeDtypeStruct((1,), jnp.int32), jax.ShapeDtypeStruct((1,), f32),
+            jax.ShapeDtypeStruct((8, LANES), jnp.int32), jax.ShapeDtypeStruct((1,), jnp.int32), jax.ShapeDtypeStruct((8, LANES), f32),
             jax.ShapeDtypeStruct(VECTOR_SHAPE, bf), jax.ShapeDtypeStruct((BOND, BOND), f32),
             jax.ShapeDtypeStruct((DEVS, 2, 256, 256), bf), jax.ShapeDtypeStruct((5, TERMS, SLAB, LANES), bf), jax.ShapeDtypeStruct((2, 2, 2, 2, 2, 128, BOND), bf),
         ),
         in_specs=[smem, hbm, hbm, vmem, hbm, hbm],
-        out_specs=(vmem, smem, smem, hbm, hbm, hbm, hbm, hbm),
+        out_specs=(hbm, smem, hbm, hbm, hbm, hbm, hbm, hbm),
         scratch_shapes=[
             pltpu.VMEM(VECTOR_SHAPE, bf),
             pltpu.VMEM((5, 2 * BOND, LANES), bf),
@@ -367,7 +395,8 @@
             pltpu.VMEM((DEVS, 2, 256, 256), bf),
             pltpu.VMEM((2, 2, 2, 2, 2, 128, BOND), bf),
             dma((8,)), dma((5,)), dma((CHUNKS,)), dma((DEVS,)), dma((DEVS,)), dma((2, DEVS)), dma((2, DEVS)),
-            dma((1, 3, 7)), dma((1, 3, 7)), dma((1, 8)), dma((1, 8)),
+            dma((1, 3, 7)), dma((1, 3, 7)), dma((1, 8)), dma((1, 8)), dma((2, 8)),
+            pltpu.VMEM((8, LANES), jnp.int32), pltpu.VMEM((8, LANES), f32),
         ],
         compiler_params=pltpu.CompilerParams(collective_id=0, has_side_effects=True, vmem_limit_bytes=67043328),
     )(flags, psi, psi.reshape(BOND * PAIR, BOND), pair_loc, right_loc.reshape(2 * BOND, BOND), left_loc)
@@ -420,15 +449,17 @@
 
     def dots(fn, count):
         def body(g, tots):
-            rows = pl.ds(pl.multiple_of(g * 16, 16), 16)
+            vals = fn(pl.ds(pl.multiple_of(g * 32, 32), 32))
             out = []
-            for tot, val in zip(tots, fn(rows)):
-                for r in range(2):
+            for n, val in enumerate(vals):
+                two = [tots[2 * n], tots[2 * n + 1]]
+                for r in range(4):
                     for c in range(5):
-                        tot = tot + val[8 * r:8 * r + 8, 128 * c:128 * c + 128]
-                out.append(tot)
+                        two[r % 2] = two[r % 2] + val[8 * r:8 * r + 8, 128 * c:128 * c + 128]
+                out += two
             return tuple(out)
-        return lax.fori_loop(0, 40, body, (jnp.zeros((8, LANES), f32),) * count)
+        tots = lax.fori_loop(0, 20, body, (jnp.zeros((8, LANES), f32),) * (2 * count))
+        return [tots[2 * n] + tots[2 * n + 1] for n in range(count)]
 
     def write_u():
         for ch in range(CHUNKS):
@@ -441,32 +472,41 @@
                 dst[48:64] = cur[256 + 32 * i + 16:256 + 32 * i + 32, lanes].astype(bf)
                 dst[64:80] = cur[512 + 16 * i:512 + 16 * i + 16, lanes].astype(bf)
 
+    def right_part(ch, par, pairs):
+        rhs = []
+        for i in pairs:
+            main = u[ch, i, :, :, :, :, 32 * par:32 * par + 32, :].reshape(512, 128)
+            tail = u[ch, i, :, :, :, :, 64:80, :].reshape(256, 128)
+            rhs.append(jnp.concatenate([main, tail], axis=0))
+        rhs = jnp.concatenate(rhs, axis=1)
+        lhs = jnp.concatenate([rc[:, 0:512], rc[:, 512 + 256 * par:768 + 256 * par]], axis=1)
+        val = jnp.dot(lhs, rhs, preferred_element_type=f32)
+        for n, i in enumerate(pairs):
+            y[2 * i + par, 0:most] = val[:, 128 * n:128 * n + 128].reshape(most, SLAB, 128).astype(bf)
+            own = u.at[ch, i, place[2], place[1], place[0], core]
+            y[2 * i + par, most, 0:32] = own[32 * par:32 * par + 32, :]
+            y[2 * i + par, most, 32:40] = own[64 + 8 * par:72 + 8 * par, :]
+
     def right_phase(ch, middle):
         for par in range(2):
             if par == 1:
                 middle()
-            rhs = []
-            for i in range(8):
-                main = u[ch, i, :, :, :, :, 32 * par:32 * par + 32, :].reshape(512, 128)
-                tail = u[ch, i, :, :, :, :, 64:80, :].reshape(256, 128)
-                rhs.append(jnp.concatenate([main, tail], axis=0))
-            rhs = jnp.concatenate(rhs, axis=1)
-            lhs = jnp.concatenate([rc[:, 0:512], rc[:, 512 + 256 * par:768 + 256 * par]], axis=1)
-            val = jnp.dot(lhs, rhs, preferred_element_type=f32)
-            for i in range(8):
-                y[2 * i + par, 0:most] = val[:, 128 * i:128 * i + 128].reshape(most, SLAB, 128).astype(bf)
-                own = u.at[ch, i, place[2], place[1], place[0], core]
-                y[2 * i + par, most, 0:32] = own[32 * par:32 * par + 32, :]
-                y[2 * i + par, most, 32:40] = own[64 + 8 * par:72 + 8 * par, :]
+            if most < TERMS:
+                right_part(ch, par, range(8))
+            else:
+                @pl.loop(0, 4)
+                def _(g):
+                    right_part(ch, par, [2 * g, 2 * g + 1])
 
     def pair_left_phase(ch, zb, half_done):
         low_rows = (iota((256, 256), 0) & 15) < 8
-
-        @pl.loop(0, 2)
+        deep = 8 if most < TERMS else 4
+
+        @pl.loop(0, DEVS // deep)
         def _(g):
-            for s in range(8):
-                k = g * 8 + s
-                first, second = [table[0 if most == FEW else 2, 2 * k + t] for t in range(2)]
+            for s in range(deep):
+                k = g * deep + s
+                first, second = [table[TABLE_ROW[most], 2 * k + t] for t in range(2)]
 
                 def tile(at, row):
                     return y[:, at, row:row + 16, :].reshape(256, 128)
@@ -482,12 +522,16 @@
                 zb[s, 0:256, 128:256] = z34[:, 0:128]
                 zb[s, 256:512, 128:256] = z34[:, 128:256]
                 zb[s, 512:640, 128:256] = z2[:, 1].reshape(128, 128).astype(bf)
-            lhs = jnp.concatenate([zb[s] for s in range(8)], axis=1)
+            lhs = jnp.concatenate([zb[s] for s in range(deep)], axis=1)
             rows = pl.ds(pl.multiple_of(ch * 128, 128), 128)
-            rhs = jnp.concatenate([lft[g, s // 4, s // 2 % 2, s % 2, t, rows, :] for s in range(8) for t in range(2)], axis=0)
-            acc[...] += jnp.dot(lhs, rhs, preferred_element_type=f32)
-
-            @pl.when(g == 0)
+            rhs = []
+            for s in range(deep):
+                for t in range(2):
+                    at = (g, s // 4, s // 2 % 2) if deep == 8 else (lax.div(g, 2), lax.rem(g, 2), s // 2)
+                    rhs.append(lft[at + (s % 2, t, rows)])
+            acc[...] += jnp.dot(lhs, jnp.concatenate(rhs, axis=0), preferred_element_type=f32)
+
+            @pl.when(g == 8 // deep - 1)
             def _():
                 half_done()
 
@@ -627,6 +671,8 @@
                 @pl.when((j == 0) & (ch > 0))
                 def _():
                     def take(view, spot):
+                        if spot.ch > 0:
+                            mirror_left(spot.ch - 1)
                         net.take_pairs(view, spot)
                         net.take_last(view, spot)
 
@@ -643,7 +689,6 @@
 
                 def left_ready(view, spot):
                     if spot.ch > 0:
-                        mirror_left(spot.ch - 1)
                         net.chunk_ready(view, spot)
 
                 for_left(ch, left_ready)
@@ -686,14 +731,15 @@
                 for_left(ch + 1, advance)
                 for_left(ch + 2, net.own_out)
 
-        @pl.loop(0, CHUNKS)
-        def _(ch):
-            @pl.when((j == 0) & (ch > 0))
-            def _():
-                for_left(ch, net.drain_sends)
-
-            @pl.when(later)
-            def _():
+        @pl.when(j == 0)
+        def _():
+            for c in range(1, CHUNKS):
+                net.drain_sends(left_view, net.at(c))
+
+        @pl.when(later)
+        def _():
+            @pl.loop(0, CHUNKS)
+            def _(ch):
                 net.drain_sends(vec_view, net.at(ch))
 
         @pl.when(j == 0)
@@ -736,9 +782,9 @@
 
         @pl.when(j + 1 < LANCZOS_STEPS)
         def _():
-            @pl.loop(0, 40)
+            @pl.loop(0, 20)
             def _(g):
-                rows = pl.ds(pl.multiple_of(g * 16, 16), 16)
+                rows = pl.ds(pl.multiple_of(g * 32, 32), 32)
                 v = cur[rows, :]
                 prev[rows, :] = v
                 cur[rows, :] = (acc[rows, :] - extra * v) / beta
@@ -812,7 +858,7 @@
         alpha_out[n] = alphas[0, n]
         beta_out[n] = betas[0, n]
     rows_load.wait()
-    dst[0] = rows[...] / norm[0]
+    dst[0] = rows[...] / norm[0, 0]
     store(0).start()
 
     @pl.loop(0, LANCZOS_STEPS - 1)
@@ -855,8 +901,8 @@
 def solution(mesh):
     def device_body(wavefunction, left_loc, pair_loc, right_loc, flag_loc):
         table, few, norm, *operands = prepare(flag_loc, wavefunction, pair_loc, right_loc, left_loc)
-        few_full, all_full = functools.partial(run_lanczos, FEW), functools.partial(run_lanczos, TERMS)
-        vecs, alphas, betas = lax.cond(few[0] == 1, few_full, all_full, table, *operands, left_loc)
+        k16, k20, k32 = [functools.partial(run_lanczos, most) for most in (FEWER, FEW, TERMS)]
+        vecs, alphas, betas = lax.switch(few[0], [k20, k32], table, *operands, left_loc)
         return place_outputs(norm, alphas, betas, wavefunction, vecs)
 
     return jax.shard_map(device_body, mesh=mesh, in_specs=(P(), P(AXIS_NAME), P(AXIS_NAME), P(AXIS_NAME), P(AXIS_NAME)), out_specs=(P(None, AXIS_NAME), P(), P()), check_vma=False)

time: 505 us -> 498 us (0.986)
  Pallas kernels: 502 us -> 495 us
    pallas_call x1, Pallas kernels: 440 us -> 434 us  [run_lanczos(): pl.pallas_call(functools.partial(lanczos_kernel, most), out_shape=(jax.Sh...]
where the time goes in v5:
time: 498 us; the launch traced here: 497 us
  Pallas kernels  495 us (99%)
    pallas_call x1, Pallas kernels, run_lanczos(): pl.pallas_call(functools.partial(lanczos_kernel, most), out_shape=(jax.Sh...  434 us
    pallas_call x1, Pallas kernels, prepare(): pl.pallas_call(prep_kernel, out_shape=(jax.ShapeDtypeStruct((8, LANES), j...  49 us
    pallas_call x1, Pallas kernels, place_outputs(): pl.pallas_call(place_kernel, out_shape=(jax.ShapeDtypeStruct((LANCZOS_STE...  11.3 us

profile of v5, /device:TPU:0, one launch (start us, length us, event | category | flops | bytes accessed | tf_op | source)
XLA Modules:
  0.0 497.3 jit_solution(16873393057632464852)
XLA Ops:
  0.6 49.0 %shard_map.76 = (s32[8,128]{1,0:T(8,128)}, s32[1]{0:T(128)}, f32[8,128]{1,0:T(8,128)}, bf16[5,8,2,2,2,2,80,128]{7,6,5,4,3,2,1,0:T(8,128)(2,1)}, f32[640,640]{1,0...) custom-call(s32[2]{0:T(128)} %flags.1, ...), custom_call_target="tpu_custom_call" | custom-call | tf_op jit(solution)/shard_map/pallas_call | solution.py:379
  50.2 434.9 %conditional.1 = ((f32[6,16,40,640]{3,2,1,0:T(8,128)}, f32[1,8]{1,0:T(1,128)}, f32[1,8]{1,0:T(1,128)})) conditional(s32[]{:T(128)} %bitcast.2, (s32[8,128]{1,0:T(8,128)}, bf16[5,8,2,2,2,2,80,128]{7,6,5,4,3,2,1,0:T(8,128)(2,1)}, f32[640,640]{1,0:T(8,128)}, bf16[16,2,256,256]{3,2,1,0:T(8,128)(2,1)}, bf16[5,32,40,128]{3,2,1,0:T(8,128)(2,1)}, ...), branch_computations={%region_0.0_spmd, %region_1.0_spmd} | conditional | bytes 8 | solution.py:905
  50.4 434.5 %branch_0_fun.1 = (f32[6,16,40,640]{3,2,1,0:T(8,128)}, f32[1,8]{1,0:T(1,128)}, f32[1,8]{1,0:T(1,128)}) custom-call(s32[8,128]{1,0:T(8,128)} %get-tuple-element.28.table, bf16[5,8,2,2,2,2,80,128]{7,6,5,4,3,2,1,0:T(8,128)(2,1)} %get-tuple-element.29.u_hbm, f32[640,640]{1,0:T(8,128)} %get-tuple-element.30.slab_hbm, ...), custom_call_target="tpu_custom_call" | custom-call | tf_op jit(solution)/shard_map/cond/branch_0_fun/pallas_call | solution.py:807
  485.2 0.0 copy-start
  485.2 0.7 copy-done
  485.8 11.3 %shard_map.77 = (f32[7,40,16,640]{3,2,1,0:T(8,128)}, f32[6]{0:T(128)}, f32[6]{0:T(128)}) custom-call(f32[8,128]{1,0:T(8,128)S(1)} %copy-done, f32[1,8]{1,0:T(1,128)} %get-tuple-element.64.alphas, f32[1,8]{1,0:T(1,128)} %get-tuple-element.65.betas, f32[640,16,640]{2,1,0:T(8,128)} %psi.3, f32[6,16,40,640]{3,2,1,0:T(8,128)} %get-tuple-element.66.gathered), custom_call_target="tpu_custom_call" | custom-call | tf_op jit(solution)/shard_map/pallas_call | solution.py:886
Async XLA Ops:
  485.2 0.7 copy-start

commit v6 on v5

--- a/solution.py
+++ b/solution.py
@@ -327,7 +327,7 @@
     holder = jnp.sum(jnp.where(rank_down == lane.astype(f32), full * term.astype(f32), 0.0), axis=0, keepdims=True)
     small_i[...] = jnp.where(row == 1, holder, jnp.where(in_lanes > 0.5, rank, jnp.where(row == 0, FEWER, jnp.where(row == 2, FEW, TERMS)).astype(f32))).astype(jnp.int32)
     count = jnp.sum(in_lanes)
-    few[0] = jnp.where(count < FEW + 0.5, 0, 1)
+    few[0] = jnp.where(count < FEWER + 0.5, 2, jnp.where(count < FEW + 0.5, 1, 0))
     table_store = pltpu.make_async_copy(small_i, table, load_sem.at[7])
     table_store.start()
     pl.run_scoped(functools.partial(start_vector, norm), pltpu.VMEM((5, 128, 8, LANES), f32), pltpu.VMEM((8, 256, LANES), f32))
@@ -461,16 +461,16 @@
         tots = lax.fori_loop(0, 20, body, (jnp.zeros((8, LANES), f32),) * (2 * count))
         return [tots[2 * n] + tots[2 * n + 1] for n in range(count)]
 
-    def write_u():
-        for ch in range(CHUNKS):
-            lanes = slice(128 * ch, 128 * ch + 128)
-            for i in range(8):
-                dst = u.at[ch, i, place[2], place[1], place[0], core]
-                dst[0:16] = cur[32 * i:32 * i + 16, lanes].astype(bf)
-                dst[16:32] = cur[256 + 32 * i:256 + 32 * i + 16, lanes].astype(bf)
-                dst[32:48] = cur[32 * i + 16:32 * i + 32, lanes].astype(bf)
-                dst[48:64] = cur[256 + 32 * i + 16:256 + 32 * i + 32, lanes].astype(bf)
-                dst[64:80] = cur[512 + 16 * i:512 + 16 * i + 16, lanes].astype(bf)
+    def next_vector(ch, extra, beta):
+        lanes = pl.ds(pl.multiple_of(128 * ch, 128), 128)
+        for i in range(8):
+            dst = u.at[ch, i, place[2], place[1], place[0], core]
+            for n, start in enumerate((32 * i, 256 + 32 * i, 32 * i + 16, 256 + 32 * i + 16, 512 + 16 * i)):
+                v = cur[start:start + 16, lanes]
+                new = (acc[start:start + 16, lanes] - extra * v) / beta
+                prev[start:start + 16, lanes] = v
+                cur[start:start + 16, lanes] = new
+                dst[16 * n:16 * n + 16] = new.astype(bf)
 
     def right_part(ch, par, pairs):
         rhs = []
@@ -623,7 +623,6 @@
         @pl.when(later)
         def _():
             zero, one = net.at(0), net.at(1)
-            net.own_out(vec_view, zero)
             turn(cur, turned)
             own_copy(turned, j - 1).start()
             net.relay_first(vec_view, zero)
@@ -731,6 +730,11 @@
                 for_left(ch + 1, advance)
                 for_left(ch + 2, net.own_out)
 
+                @pl.when(ch == CHUNKS - 2)
+                def _():
+                    slab_load.wait()
+                    send_partial(0, dots(lambda rows: (acc[rows, :] * cur[rows, :],), 1))
+
         @pl.when(j == 0)
         def _():
             for c in range(1, CHUNKS):
@@ -744,12 +748,7 @@
 
         @pl.when(j == 0)
         def _():
-            slab_load.wait()
-
-        @pl.when(j == 0)
-        def _():
-            send_partial(0, dots(lambda rows: (acc[rows, :] * cur[rows, :],), 1))
-            betas[0, LANCZOS_STEPS + 1] = total_of(0, 1)[0]
+            betas[0, LANCZOS_STEPS + 1] = total_of(0, 1)[0] * (CHUNKS / (CHUNKS - 1))
 
         shift = betas[0, LANCZOS_STEPS + 1]
 
@@ -782,14 +781,12 @@
 
         @pl.when(j + 1 < LANCZOS_STEPS)
         def _():
-            @pl.loop(0, 20)
-            def _(g):
-                rows = pl.ds(pl.multiple_of(g * 32, 32), 32)
-                v = cur[rows, :]
-                prev[rows, :] = v
-                cur[rows, :] = (acc[rows, :] - extra * v) / beta
-
-            write_u()
+            next_vector(0, extra, beta)
+            net.own_out(vec_view, net.at(0))
+
+            @pl.loop(1, CHUNKS)
+            def _(ch):
+                next_vector(ch, extra, beta)
 
         return beta
 
@@ -826,7 +823,7 @@
     )(table, u_hbm, slab_hbm, wi_hbm, right_hbm, first_left, left_loc)
 
 
-def place_kernel(norm, alphas, betas, psi, gathered, krylov, alpha_out, beta_out, rows, src, dst, load_sem, store_sem):
+def place_kernel(alphas, betas, norm_hbm, psi, gathered, krylov, alpha_out, beta_out, norm, rows, src, dst, load_sem, store_sem):
     me = lax.axis_index(AXIS_NAME)
 
     def load(vec):
@@ -847,33 +844,40 @@
         skip, rest = SLAB * q // 128, SLAB * q % 128
         if rest:
             tiles = [pltpu.roll(tile, 128 - rest, 1) for tile in tiles]
-        tiles = [tiles[(t + skip) % 5] if not rest else jnp.where(lane < 128 - rest, tiles[(t + skip) % 5], tiles[(t + skip + 1) % 5]) for t in range(5)]
-        return jnp.concatenate(tiles, axis=1)
+        return [tiles[(t + skip) % 5] if not rest else jnp.where(lane < 128 - rest, tiles[(t + skip) % 5], tiles[(t + skip + 1) % 5]) for t in range(5)]
+
+    def blocks(vec):
+        for r in range(0, SLAB, 8):
+            for half in range(0, PAIR, 8):
+                found = [placed(vec, r, q) for q in range(half, half + 8)]
+                for t in range(5):
+                    block = jnp.stack([tiles[t] for tiles in found], axis=0).transpose(1, 0, 2)
+                    yield (slice(r, r + 8), slice(half, half + 8), slice(128 * t, 128 * t + 128)), block
 
     rows_load = pltpu.make_async_copy(psi.at[pl.ds(me * SLAB, SLAB)], rows, load_sem.at[LANCZOS_STEPS])
     rows_load.start()
+    norm_load = pltpu.make_async_copy(norm_hbm, norm, load_sem.at[LANCZOS_STEPS + 1])
+    norm_load.start()
     for vec in range(LANCZOS_STEPS):
         load(vec).start()
     for n in range(LANCZOS_STEPS):
         alpha_out[n] = alphas[0, n]
         beta_out[n] = betas[0, n]
     rows_load.wait()
+    norm_load.wait()
     dst[0] = rows[...] / norm[0, 0]
     store(0).start()
 
     @pl.loop(0, LANCZOS_STEPS - 1)
     def _(vec):
         load(vec).wait()
-        for r in range(0, SLAB, 8):
-            for q in range(PAIR):
-                dst[vec + 1, r:r + 8, q, :] = placed(vec, r, q)
+        for at, block in blocks(vec):
+            dst[(vec + 1,) + at] = block
         store(vec + 1).start()
 
     load(LANCZOS_STEPS - 1).wait()
-    for r in range(0, SLAB, 8):
-        for q in range(PAIR):
-            before = dst[LANCZOS_STEPS - 1, r:r + 8, q, :]
-            dst[LANCZOS_STEPS, r:r + 8, q, :] = (placed(LANCZOS_STEPS - 1, r, q) - betas[0, LANCZOS_STEPS] * before) / betas[0, LANCZOS_STEPS - 1]
+    for at, block in blocks(LANCZOS_STEPS - 1):
+        dst[(LANCZOS_STEPS,) + at] = (block - betas[0, LANCZOS_STEPS] * dst[(LANCZOS_STEPS - 1,) + at]) / betas[0, LANCZOS_STEPS - 1]
     store(LANCZOS_STEPS).start()
     for vec in range(LANCZOS_STEPS + 1):
         store(vec).wait()
@@ -886,23 +890,24 @@
     return pl.pallas_call(
         place_kernel,
         out_shape=(jax.ShapeDtypeStruct((LANCZOS_STEPS + 1, SLAB, PAIR, BOND), f32), jax.ShapeDtypeStruct((LANCZOS_STEPS,), f32), jax.ShapeDtypeStruct((LANCZOS_STEPS,), f32)),
-        in_specs=[smem, smem, smem, hbm, hbm],
+        in_specs=[smem, smem, hbm, hbm, hbm],
         out_specs=(hbm, smem, smem),
         scratch_shapes=[
+            pltpu.SMEM((8, LANES), f32),
             pltpu.VMEM((SLAB, PAIR, BOND), f32),
             pltpu.VMEM((LANCZOS_STEPS, DEVS, SLAB, BOND), f32),
             pltpu.VMEM((LANCZOS_STEPS + 1, SLAB, PAIR, BOND), f32),
-            dma((LANCZOS_STEPS + 1,)), dma((LANCZOS_STEPS + 1,)),
+            dma((LANCZOS_STEPS + 2,)), dma((LANCZOS_STEPS + 1,)),
         ],
-        compiler_params=pltpu.CompilerParams(vmem_limit_bytes=40 * 1024 * 1024),
-    )(norm, alphas, betas, wavefunction, gathered)
+        compiler_params=pltpu.CompilerParams(vmem_limit_bytes=67043328),
+    )(alphas, betas, norm, wavefunction, gathered)
 
 
 def solution(mesh):
     def device_body(wavefunction, left_loc, pair_loc, right_loc, flag_loc):
         table, few, norm, *operands = prepare(flag_loc, wavefunction, pair_loc, right_loc, left_loc)
-        k16, k20, k32 = [functools.partial(run_lanczos, most) for most in (FEWER, FEW, TERMS)]
-        vecs, alphas, betas = lax.switch(few[0], [k20, k32], table, *operands, left_loc)
+        kernels = [functools.partial(run_lanczos, most) for most in (TERMS, FEW, FEWER)]
+        vecs, alphas, betas = lax.switch(few[0], kernels, table, *operands, left_loc)
         return place_outputs(norm, alphas, betas, wavefunction, vecs)
 
     return jax.shard_map(device_body, mesh=mesh, in_specs=(P(), P(AXIS_NAME), P(AXIS_NAME), P(AXIS_NAME), P(AXIS_NAME)), out_specs=(P(None, AXIS_NAME), P(), P()), check_vma=False)

time: 498 us -> 489 us (0.982)
  Pallas kernels: 495 us -> 486 us
    pallas_call x1, Pallas kernels: 434 us -> 427 us  [run_lanczos(): pl.pallas_call(functools.partial(lanczos_kernel, most), out_shape=(jax.Sh...]
where the time goes in v6:
time: 489 us
  Pallas kernels  486 us (99%)
    pallas_call x1, Pallas kernels, run_lanczos(): pl.pallas_call(functools.partial(lanczos_kernel, most), out_shape=(jax.Sh...  427 us
    pallas_call x1, Pallas kernels, prepare(): pl.pallas_call(prep_kernel, out_shape=(jax.ShapeDtypeStruct((8, LANES), j...  49 us
    pallas_call x1, Pallas kernels, place_outputs(): pl.pallas_call(place_kernel, out_shape=(jax.ShapeDtypeStruct((LANCZOS_STE...  10 us

profile of v6, /device:TPU:0, one launch (start us, length us, event | category | flops | bytes accessed | tf_op | source)
XLA Modules:
  0.0 488.9 jit_solution(17852183749022209287)
XLA Ops:
  0.6 49.0 %shard_map.76 = (s32[8,128]{1,0:T(8,128)}, s32[1]{0:T(128)}, f32[8,128]{1,0:T(8,128)}, bf16[5,8,2,2,2,2,80,128]{7,6,5,4,3,2,1,0:T(8,128)(2,1)}, f32[640,640]{1,0...) custom-call(s32[2]{0:T(128)} %flags.1, ...), custom_call_target="tpu_custom_call" | custom-call | tf_op jit(solution)/shard_map/pallas_call | solution.py:379
  50.3 428.4 %conditional.1 = ((f32[6,16,40,640]{3,2,1,0:T(8,128)}, f32[1,8]{1,0:T(1,128)}, f32[1,8]{1,0:T(1,128)})) conditional(s32[]{:T(128)} %bitcast.2, (s32[8,128]{1,0:T(8,128)}, bf16[5,8,2,2,2,2,80,128]{7,6,5,4,3,2,1,0:T(8,128)(2,1)}, f32[640,640]{1,0:T(8,128)}, bf16[16,2,256,256]{3,2,1,0:T(8,128)(2,1)}, ...), branch_computations={%region_0.0_spmd, %region_1.0_spmd, %region_2.0_spmd} | conditional | bytes 8 | solution.py:910
  51.1 427.4 %branch_2_fun.1 = (f32[6,16,40,640]{3,2,1,0:T(8,128)}, f32[1,8]{1,0:T(1,128)}, f32[1,8]{1,0:T(1,128)}) custom-call(s32[8,128]{1,0:T(8,128)} %get-tuple-element.56.table, bf16[5,8,2,2,2,2,80,128]{7,6,5,4,3,2,1,0:T(8,128)(2,1)} %get-tuple-element.57.u_hbm, f32[640,640]{1,0:T(8,128)} %get-tuple-element.58.slab_hbm, ...), custom_call_target="tpu_custom_call" | custom-call | tf_op jit(solution)/shard_map/cond/branch_2_fun/pallas_call | solution.py:804
  478.7 10.0 %shard_map.77 = (f32[7,40,16,640]{3,2,1,0:T(8,128)}, f32[6]{0:T(128)}, f32[6]{0:T(128)}) custom-call(f32[1,8]{1,0:T(1,128)} %get-tuple-element.84.alphas, f32[1,8]{1,0:T(1,128)} %get-tuple-element.85.betas, f32[8,128]{1,0:T(8,128)} %get-tuple-element.86.norm_hbm, f32[640,16,640]{2,1,0:T(8,128)} %psi.3, f32[6,16,40,640]{3,2,1,0:T(8,128)} %get-tuple-element.87.gathered), custom_call_target="tpu_custom_call" | custom-call | tf_op jit(solution)/shard_map/pallas_call | solution.py:890

commit v7 on v6

--- a/solution.py
+++ b/solution.py
@@ -14,8 +14,8 @@
 DEVS = 16
 SLAB = BOND // DEVS
 CHUNKS = 5
-FEWER, FEW = 16, 20
-TABLE_ROW = {16: 0, 20: 2, 32: 3}
+FEWER, FEW = 20, 24
+TABLE_ROW = {20: 0, 24: 2, 32: 3}
 LANES = 128
 VEC_SIZE = BOND * PAIR * BOND
 bf = jnp.bfloat16
@@ -494,13 +494,13 @@
             if most < TERMS:
                 right_part(ch, par, range(8))
             else:
-                @pl.loop(0, 4)
-                def _(g):
-                    right_part(ch, par, [2 * g, 2 * g + 1])
+                @pl.loop(0, 8)
+                def _(i):
+                    right_part(ch, par, [i])
 
     def pair_left_phase(ch, zb, half_done):
         low_rows = (iota((256, 256), 0) & 15) < 8
-        deep = 8 if most < TERMS else 4
+        deep = 8 if most < TERMS else 2
 
         @pl.loop(0, DEVS // deep)
         def _(g):
@@ -527,7 +527,7 @@
             rhs = []
             for s in range(deep):
                 for t in range(2):
-                    at = (g, s // 4, s // 2 % 2) if deep == 8 else (lax.div(g, 2), lax.rem(g, 2), s // 2)
+                    at = (g, s // 4, s // 2 % 2) if deep == 8 else (lax.div(g, 4), lax.rem(lax.div(g, 2), 2), lax.rem(g, 2))
                     rhs.append(lft[at + (s % 2, t, rows)])
             acc[...] += jnp.dot(lhs, jnp.concatenate(rhs, axis=0), preferred_element_type=f32)
 

time: 489 us -> 491 us (level)
  no operation moved by 1% of the time
where the time goes in v7:
time: 491 us
  Pallas kernels  488 us (99%)
    pallas_call x1, Pallas kernels, run_lanczos(): pl.pallas_call(functools.partial(lanczos_kernel, most), out_shape=(jax.Sh...  429 us
    pallas_call x1, Pallas kernels, prepare(): pl.pallas_call(prep_kernel, out_shape=(jax.ShapeDtypeStruct((8, LANES), j...  49 us
    pallas_call x1, Pallas kernels, place_outputs(): pl.pallas_call(place_kernel, out_shape=(jax.ShapeDtypeStruct((LANCZOS_STE...  10 us

profile of v7, /device:TPU:0, one launch (start us, length us, event | category | flops | bytes accessed | tf_op | source)
XLA Modules:
  0.0 490.7 jit_solution(3138562473526802344)
XLA Ops:
  0.6 49.0 %shard_map.76 = (s32[8,128]{1,0:T(8,128)}, s32[1]{0:T(128)}, f32[8,128]{1,0:T(8,128)}, bf16[5,8,2,2,2,2,80,128]{7,6,5,4,3,2,1,0:T(8,128)(2,1)}, f32[640,640]{1,0...) custom-call(s32[2]{0:T(128)} %flags.1, ...), custom_call_target="tpu_custom_call" | custom-call | tf_op jit(solution)/shard_map/pallas_call | solution.py:379
  50.3 430.2 %conditional.1 = ((f32[6,16,40,640]{3,2,1,0:T(8,128)}, f32[1,8]{1,0:T(1,128)}, f32[1,8]{1,0:T(1,128)})) conditional(s32[]{:T(128)} %bitcast.2, (s32[8,128]{1,0:T(8,128)}, bf16[5,8,2,2,2,2,80,128]{7,6,5,4,3,2,1,0:T(8,128)(2,1)}, f32[640,640]{1,0:T(8,128)}, bf16[16,2,256,256]{3,2,1,0:T(8,128)(2,1)}, ...), branch_computations={%region_0.0_spmd, %region_1.0_spmd, %region_2.0_spmd} | conditional | bytes 8 | solution.py:910
  51.0 429.2 %branch_2_fun.1 = (f32[6,16,40,640]{3,2,1,0:T(8,128)}, f32[1,8]{1,0:T(1,128)}, f32[1,8]{1,0:T(1,128)}) custom-call(s32[8,128]{1,0:T(8,128)} %get-tuple-element.56.table, bf16[5,8,2,2,2,2,80,128]{7,6,5,4,3,2,1,0:T(8,128)(2,1)} %get-tuple-element.57.u_hbm, f32[640,640]{1,0:T(8,128)} %get-tuple-element.58.slab_hbm, ...), custom_call_target="tpu_custom_call" | custom-call | tf_op jit(solution)/shard_map/cond/branch_2_fun/pallas_call | solution.py:804
  480.5 10.0 %shard_map.77 = (f32[7,40,16,640]{3,2,1,0:T(8,128)}, f32[6]{0:T(128)}, f32[6]{0:T(128)}) custom-call(f32[1,8]{1,0:T(1,128)} %get-tuple-element.84.alphas, f32[1,8]{1,0:T(1,128)} %get-tuple-element.85.betas, f32[8,128]{1,0:T(8,128)} %get-tuple-element.86.norm_hbm, f32[640,16,640]{2,1,0:T(8,128)} %psi.3, f32[6,16,40,640]{3,2,1,0:T(8,128)} %get-tuple-element.87.gathered), custom_call_target="tpu_custom_call" | custom-call | tf_op jit(solution)/shard_map/pallas_call | solution.py:890
